TPU v7x, 32 devices: a whole 2x2x4 slice. The times are simulated.
32 devices in a mesh: gx: 2 (over y), gz: 4 (over x, core), ga: 4 (over z).
Axes of the slice: x: 2, y: 2, z: 4, core: 2. Of those that a mesh axis runs over, the one named last changes fastest.
Arguments:
- right_side: float32 [32, 128, 512], P('gx', 'ga', 'gz'), may hold values from -60 to 60, as said below
- diagonal: float32 [32, 128, 512], P('gx', 'ga', 'gz'), may hold values from 0.02 to 1
- element_features: bfloat16 [256, 4096], P(None, ('gx', 'gz', 'ga')), may hold values from -6 to 6
- sample_bank: bfloat16 [256, 131072], P(None, ('gx', 'gz', 'ga')), may hold values from -6 to 6
- target_bank: bfloat16 [6, 131072], P(None, ('gx', 'gz', 'ga')), may hold values from -6 to 6
- patch_index: int32 [65536], P(('gx', 'gz', 'ga')), may hold values from 0 to 4095
- w_first: bfloat16 [256, 256], replicated, may hold values from -0.375 to 0.375
- w_second: bfloat16 [256, 256], replicated, may hold values from -0.375 to 0.375
- w_third: bfloat16 [6, 256], replicated, may hold values from -0.375 to 0.375
Outputs:
- pressure: float32 [32, 128, 512], P('gx', 'ga', 'gz')
- residual: float32 [32, 128, 512], P('gx', 'ga', 'gz')
- step_first: float32 [256, 256], replicated
- step_second: float32 [256, 256], replicated
- step_third: float32 [6, 256], replicated
Inputs may be any that keep to these rules, and one draw needn't show every extreme that they name: `right_side`: grows in magnitude along the first dimension. `patch_index`: each entry names a column of the sample_bank and target_bank block that lies on the same device as the entry.
All inputs are finite; a program needn't handle non-finite values.
Results may differ from a plain program's by a relative error of at most 0.0004.
The roundings to bfloat16 on the way count: a program that leaves them out, or rounds other values in their place, can miss the bound.
Values sent between devices are 32-bit elements; how exact they have to be, the bound alone decides.
A program may use at most 64 MiB of HBM per device.

v0:
```python
import functools

import jax
import jax.numpy as jnp
from jax import lax
from jax.experimental import pallas as pl
from jax.experimental.pallas import tpu as pltpu
from jax.sharding import PartitionSpec as P

EL = 8
ITERS = 12
TILE = 512
PHASES = (("gx", "gz"), ("ga",))
AXES = ("gx", "gz", "ga")

taps = (1.6, -0.2, 8.0 / 315.0, -1.0 / 560.0)
center = 3.0 * 205.0 / 72.0
epsilon = 1e-06
MESH = pl.DeviceIdType.MESH
F32 = jnp.float32
BF16 = jnp.bfloat16


def dot(a, b, dims=((1,), (0,)), precision=None):
    return lax.dot_general(a, b, (dims, ((), ())), preferred_element_type=F32, precision=precision)


def sigmoid(v):
    return 1.0 / (1.0 + jnp.exp(-v))


def grad_kernel(bank, target, index, w1, w2, w3, grads, counts):
    step = pl.program_id(0)
    rows = TILE // 128

    @pl.when(step == 0)
    def _():
        samples = index.shape[1]
        groups = counts.shape[0]
        ids = index[...]
        high = lax.broadcasted_iota(jnp.int32, (groups, samples), 0) == (ids // 128)
        low = lax.broadcasted_iota(jnp.int32, (128, samples), 0) == (ids % 128)
        counts[...] = dot(
            jnp.where(high, 1.0, 0.0).astype(BF16),
            jnp.where(low, 1.0, 0.0).astype(BF16),
            ((1,), (1,)),
        )
        grads[...] = jnp.zeros_like(grads)

    weight = jnp.concatenate([counts[pl.ds(step * rows + j, 1), :] for j in range(rows)], axis=1)
    x = bank[...]
    ch = x.shape[0]
    stress = target.shape[0]
    a1, a2, a3 = w1[...], w2[...], w3[...]
    l1 = dot(a1, x)
    s1 = sigmoid(l1)
    h1 = (l1 * s1).astype(BF16)
    l2 = dot(a2, h1)
    s2 = sigmoid(l2)
    h2 = (l2 * s2).astype(BF16)
    error = (dot(a3, h2) - target[...].astype(F32)).astype(BF16)

    def weighted(delta, right):
        scaled = delta.astype(F32) * weight
        upper = scaled.astype(BF16)
        lower = (scaled - upper.astype(F32)).astype(BF16)
        return dot(upper, right, ((1,), (1,))) + dot(lower, right, ((1,), (1,)))

    grads[2 * ch : 2 * ch + stress] += weighted(error, h2)
    d2 = (dot(a3, error, ((0,), (0,))) * (s2 * (1.0 + l2 * (1.0 - s2)))).astype(BF16)
    grads[ch : 2 * ch] += weighted(d2, h1)
    d1 = (dot(a2, d2, ((0,), (0,))) * (s1 * (1.0 + l1 * (1.0 - s1)))).astype(BF16)
    grads[:ch] += weighted(d1, x)


def closure_gradients(bank, target, index, w1, w2, w3, rows):
    ch, columns = bank.shape
    stress = target.shape[0]
    whole = pl.BlockSpec(memory_space=pltpu.VMEM)
    fixed = lambda shape: pl.BlockSpec(shape, lambda i: (0, 0))
    return pl.pallas_call(
        grad_kernel,
        grid=(columns // TILE,),
        in_specs=[
            pl.BlockSpec((ch, TILE), lambda i: (0, i)),
            pl.BlockSpec((stress, TILE), lambda i: (0, i)),
            whole,
            whole,
            whole,
            whole,
        ],
        out_specs=fixed((rows, ch)),
        out_shape=jax.ShapeDtypeStruct((rows, ch), F32),
        scratch_shapes=[pltpu.VMEM((columns // 128, 128), F32)],
        compiler_params=pltpu.CompilerParams(dimension_semantics=("arbitrary",)),
        cost_estimate=pl.CostEstimate(
            flops=14 * ch * ch * columns, bytes_accessed=2 * ch * columns, transcendentals=4 * ch * columns
        ),
    )(bank, target, index.reshape(1, -1), w1, w2, w3)


def shift_offsets(sizes):
    combos = [()]
    for n in sizes:
        combos = [c + (k,) for c in combos for k in range(n)]
    return combos[1:]


def solve_kernel(
    sizes, right, diag, feats, w1, w2, w3, grads, press, resid, step1, step2, step3,
    mp, nb, wv, zv, sv, pv, inv, yp, yr, zp, zr, ar_src, ar_dst,
    first, held, second, owned, third, full, g_send, g_recv,
    h_send, h_recv, a_send, a_recv,
):
    lx, ly, lz = right.shape
    pos = {a: lax.axis_index(a) for a in AXES}

    def coords(axes, offs, sign):
        out = {}
        for a, k in zip(axes, offs):
            n = sizes[a]
            c = pos[a] + (k if sign > 0 else n - k) if k else pos[a]
            out[a] = lax.rem(c, n) if k else c
        return out

    def flat(axes, at):
        value = 0
        for a in axes:
            value = value * sizes[a] + at[a]
        return value

    groups = []
    for axes in PHASES:
        me = flat(axes, pos)
        peers = []
        for offs in shift_offsets([sizes[a] for a in axes]):
            to = {**pos, **coords(axes, offs, 1)}
            source = flat(axes, coords(axes, offs, -1))
            peers.append((to, source))
        groups.append((me, peers))

    nx, nz, na = sizes["gx"], sizes["gz"], sizes["ga"]
    share = grads.shape[0] // nz
    piece = share // na

    def block_of(iz, ia=None):
        if ia is None:
            return pl.ds(pl.multiple_of(iz * share, 8), share)
        return pl.ds(pl.multiple_of((iz * na + ia) * piece, 8), piece)

    def along(axis, k, sign):
        return coords((axis,), (k,), sign)[axis]

    def gather_copy(number, axis, k, src, dst):
        return pltpu.make_async_remote_copy(
            src_ref=src,
            dst_ref=dst,
            send_sem=g_send.at[number],
            recv_sem=g_recv.at[number],
            device_id={**pos, axis: along(axis, k, 1)},
            device_id_type=MESH,
        )

    def scatter_gz(k):
        return gather_copy(k - 1, "gz", k, grads.at[block_of(along("gz", k, 1))], first.at[k - 1])

    def scatter_ga(k):
        rows = pl.ds(pl.multiple_of(along("ga", k, 1) * piece, 8), piece)
        return gather_copy(nz - 1 + k - 1, "ga", k, held.at[rows], second.at[k - 1])

    def add_gx(k, sign=1):
        slot = pos["gx"] if sign > 0 else along("gx", k, -1)
        return gather_copy(nz + na - 2 + k - 1, "gx", k, owned, third.at[slot])

    def gather_ga(k, sign=1):
        at = pos["ga"] if sign > 0 else along("ga", k, -1)
        rows = block_of(pos["gz"], at)
        return gather_copy(nz + na + nx - 3 + k - 1, "ga", k, full.at[rows], full.at[rows])

    def gather_gz(k, sign=1):
        at = pos["gz"] if sign > 0 else along("gz", k, -1)
        rows = block_of(at)
        return gather_copy(nz + 2 * na + nx - 4 + k - 1, "gz", k, full.at[rows], full.at[rows])

    def gradient_prepare(i):
        @pl.when(i == 3)
        def _():
            total = grads[block_of(pos["gz"]), :]
            for k in range(1, nz):
                scatter_gz(k).wait_recv()
                total = total + first[k - 1]
            held[...] = total

        @pl.when(i == 4)
        def _():
            total = held[pl.ds(pl.multiple_of(pos["ga"] * piece, 8), piece), :]
            for k in range(1, na):
                scatter_ga(k).wait_recv()
                total = total + second[k - 1]
            owned[...] = total
            third[pos["gx"]] = total

        @pl.when(i == 5)
        def _():
            for k in range(1, nx):
                add_gx(k, -1).wait_recv()
            full[block_of(pos["gz"], pos["ga"]), :] = jnp.sum(third[...], axis=0)

        @pl.when(i == 6)
        def _():
            for k in range(1, na):
                gather_ga(k, -1).wait_recv()

    def gradient_send(i):
        for turn in range(3):

            @pl.when(i == turn)
            def _():
                for k in range(1 + turn, nz, 3):
                    scatter_gz(k).start()

            @pl.when(i == 6 + turn)
            def _():
                for k in range(1 + turn, nz, 3):
                    gather_gz(k).start()

        @pl.when(i == 3)
        def _():
            for k in range(1, na):
                scatter_ga(k).start()

        @pl.when(i == 4)
        def _():
            for k in range(1, nx):
                add_gx(k).start()

        @pl.when(i == 5)
        def _():
            for k in range(1, na):
                gather_ga(k).start()

    def gradient_finish():
        for k in range(1, nz):
            gather_gz(k, -1).wait_recv()
            scatter_gz(k).wait_send()
            gather_gz(k).wait_send()
        for k in range(1, na):
            scatter_ga(k).wait_send()
            gather_ga(k).wait_send()
        for k in range(1, nx):
            add_gx(k).wait_send()
        ch = step1.shape[0]
        start = 0
        for out in (step1, step2, step3):
            count = out.shape[0]
            value = full[start : start + count]
            squares = jnp.sum(jnp.sum(value * value, axis=0, keepdims=True), axis=1, keepdims=True)
            out[...] = value * lax.rsqrt(squares / (count * ch) + epsilon)
            start += count

    mp[...] = jnp.zeros_like(mp)
    yr[...] = jnp.zeros_like(yr)
    zr[...] = jnp.zeros_like(zr)

    barrier = pltpu.get_barrier_semaphore()
    total = 0
    for _, peers in groups:
        for to, _ in peers:
            pl.semaphore_signal(barrier, inc=1, device_id=to, device_id_type=MESH)
            total += 1
    pl.semaphore_wait(barrier, total)

    lane = lax.broadcasted_iota(jnp.int32, (ly, lz), 1)
    sub8 = lax.broadcasted_iota(jnp.int32, (8, lz), 0)
    row_lane = lax.broadcasted_iota(jnp.int32, (1, lz), 1)

    def halo_copies(par):
        out = []

        def add(axis, step, number, src, dst):
            copy = pltpu.make_async_remote_copy(
                src_ref=src,
                dst_ref=dst,
                send_sem=h_send.at[number],
                recv_sem=h_recv.at[par, number],
                device_id={**pos, axis: jnp.clip(pos[axis] + step, 0, sizes[axis] - 1)},
                device_id_type=MESH,
            )
            can_send = pos[axis] < sizes[axis] - 1 if step > 0 else pos[axis] > 0
            will_get = pos[axis] > 0 if step > 0 else pos[axis] < sizes[axis] - 1
            out.append((copy, can_send, will_get))

        rows = pl.ds(8, ly)
        if sizes["gx"] > 1:
            add("gx", 1, 0, mp.at[par, pl.ds(lx, 4), rows], mp.at[par, pl.ds(0, 4), rows])
            add("gx", -1, 1, mp.at[par, pl.ds(4, 4), rows], mp.at[par, pl.ds(lx + 4, 4), rows])
        if sizes["ga"] > 1:
            add("ga", 1, 2, yp.at[par], yr.at[par, 0])
            add("ga", -1, 3, yp.at[par], yr.at[par, 1])
        if sizes["gz"] > 1:
            add("gz", 1, 4, zp.at[par], zr.at[par, 0])
            add("gz", -1, 5, zp.at[par], zr.at[par, 1])
        return out

    def halo_start(par):
        for copy, can_send, _ in halo_copies(par):
            pl.when(can_send)(copy.start)

    def halo_wait(par):
        for copy, _, will_get in halo_copies(par):
            pl.when(will_get)(copy.wait_recv)

    def halo_sent(par):
        for copy, can_send, _ in halo_copies(par):
            pl.when(can_send)(copy.wait_send)

    bases = []
    base = 0
    for axes in PHASES:
        bases.append(base)
        n = 1
        for a in axes:
            n *= sizes[a]
        base += n

    def sum_copies(par, phase):
        me, peers = groups[phase]
        out = []
        for k, (to, source) in enumerate(peers):
            slot = bases[phase]
            send = pltpu.make_async_remote_copy(
                src_ref=ar_src.at[par, phase],
                dst_ref=ar_dst.at[par, slot + me],
                send_sem=a_send.at[slot + k],
                recv_sem=a_recv.at[par, slot + me],
                device_id=to,
                device_id_type=MESH,
            )
            receive = pltpu.make_async_remote_copy(
                src_ref=ar_src.at[par, phase],
                dst_ref=ar_dst.at[par, slot + source],
                send_sem=a_send.at[slot + k],
                recv_sem=a_recv.at[par, slot + source],
                device_id=to,
                device_id_type=MESH,
            )
            out.append((send, receive))
        return out

    def sum_start(par, phase, row):
        ar_src[par, phase] = row
        ar_dst[par, bases[phase] + groups[phase][0]] = row
        for send, _ in sum_copies(par, phase):
            send.start()

    def sum_wait(par, phase):
        count = len(groups[phase][1]) + 1
        for _, receive in sum_copies(par, phase):
            receive.wait_recv()
        return jnp.sum(ar_dst[par, pl.ds(bases[phase], count)], axis=0)

    def sums_sent(par):
        for phase in range(len(PHASES)):
            for send, _ in sum_copies(par, phase):
                send.wait_send()

    def stencil_local(par):
        for x in range(lx):
            v = mp[par, 4 + x, pl.ds(8, ly)]
            acc = None
            for k in range(1, 5):
                t = mp[par, 4 + x, pl.ds(8 + k, ly)] + mp[par, 4 + x, pl.ds(8 - k, ly)]
                if x + k < lx:
                    t = t + mp[par, 4 + x + k, pl.ds(8, ly)]
                if x - k >= 0:
                    t = t + mp[par, 4 + x - k, pl.ds(8, ly)]
                t = t + jnp.where(lane >= k, pltpu.roll(v, k, 1), 0.0)
                t = t + jnp.where(lane < lz - k, pltpu.roll(v, lz - k, 1), 0.0)
                t = taps[k - 1] * t
                acc = t if acc is None else acc + t
            nb[x] = acc

    def z_correction(par):
        h = jnp.where(lane % 8 < 4, zr[par, 0], zr[par, 1])
        acc = jnp.zeros((ly, lz), F32)
        place = lane % 8
        for k in range(1, 5):
            ahead = jnp.where((place >= 4) & (place - 4 < k), pltpu.roll(h, k, 1), 0.0)
            behind = jnp.where((place < 4) & (place >= 4 - k), pltpu.roll(h, lz - k, 1), 0.0)
            acc = acc + taps[k - 1] * (ahead + behind)
        return acc

    def corrected(par, x, zc):
        acc = nb[x]
        for k in range(1, 5):
            if x - k < 0:
                acc = acc + taps[k - 1] * mp[par, 4 + x - k, pl.ds(8, ly)]
            if x + k >= lx:
                acc = acc + taps[k - 1] * mp[par, 4 + x + k, pl.ds(8, ly)]
        z = pltpu.roll(zc, (2 * lz - 8 * x - 4) % lz, 1)
        acc = acc + jnp.where((lane < 4) | (lane >= lz - 4), z, 0.0)
        h = jnp.where(sub8 < 4, yr[par, 1, x], yr[par, 0, x])
        low = jnp.zeros((8, lz), F32)
        high = jnp.zeros((8, lz), F32)
        for k in range(1, 5):
            low = low + taps[k - 1] * jnp.where(sub8 < k, pltpu.roll(h, k, 0), 0.0)
            high = high + taps[k - 1] * jnp.where(sub8 >= 8 - k, pltpu.roll(h, 8 - k, 0), 0.0)
        parts = [acc[:8] + low] + ([acc[8:-8]] if ly > 16 else []) + [acc[-8:] + high]
        return jnp.concatenate(parts, axis=0)

    def publish(par, x, m, packed):
        mp[par, 4 + x, pl.ds(8, ly)] = m
        yp[par, x] = jnp.where(sub8 < 4, m[:8], m[-8:])
        turned = pltpu.roll(m, (8 * x + 4) % lz, 1)
        return jnp.where((lane >= 8 * x) & (lane < 8 * x + 8), turned, packed)

    def fold(v):
        v = jnp.sum(v, axis=0, keepdims=True)
        return v + pltpu.roll(v, lz // 2, 1)

    def pair_row(gamma, delta):
        return jnp.where(row_lane < lz // 2, fold(gamma), fold(delta))

    def unpair(row):
        gamma = jnp.sum(jnp.where(row_lane < lz // 2, row, 0.0), axis=1, keepdims=True)
        delta = jnp.sum(jnp.where(row_lane < lz // 2, 0.0, row), axis=1, keepdims=True)
        return jnp.broadcast_to(gamma, (1, lz)), jnp.broadcast_to(delta, (1, lz))

    hidden = dot(w1[...], feats[...])
    hidden = (hidden * sigmoid(hidden)).astype(BF16)
    hidden = dot(w2[...], hidden)
    hidden = (hidden * sigmoid(hidden)).astype(BF16)
    predicted = dot(w3[...], hidden)
    trace = (predicted[0:1] + predicted[1:2] + predicted[2:3]) / 3.0
    ex, ey, ez = lx // EL, ly // EL, lz // EL
    spread = jnp.where(
        lax.broadcasted_iota(jnp.int32, (lz, lz), 0) == lax.broadcasted_iota(jnp.int32, (lz, lz), 1) // EL,
        1.0,
        0.0,
    )
    lines = jnp.concatenate(
        [trace if e == 0 else pltpu.roll(trace, (lz - e * ez) % lz, 1) for e in range(ex * ey)], axis=0
    )
    forcing = dot(lines, spread, precision=lax.Precision.HIGHEST)
    packed = jnp.zeros((ly, lz), F32)
    for x in range(lx):
        line = forcing[(x // EL) * ey : (x // EL) * ey + ey]
        block = jnp.concatenate([jnp.broadcast_to(line[j : j + 1], (EL, lz)) for j in range(ey)], axis=0)
        source = right[x] + block
        scale = 1.0 / (diag[x] + center)
        inv[x] = scale
        resid[x] = source
        packed = publish(1, x, source * scale, packed)
    zp[1] = packed
    press[...] = jnp.zeros_like(press)
    zv[...] = jnp.zeros_like(zv)
    sv[...] = jnp.zeros_like(sv)
    pv[...] = jnp.zeros_like(pv)
    halo_start(1)
    stencil_local(1)
    halo_wait(1)
    zc = z_correction(1)
    packed = jnp.zeros((ly, lz), F32)
    gamma = jnp.zeros((ly, lz), F32)
    delta = jnp.zeros((ly, lz), F32)
    for x in range(lx):
        r = resid[x]
        scale = inv[x]
        u = r * scale
        w = r - corrected(1, x, zc)
        wv[x] = w
        gamma = gamma + r * u
        delta = delta + w * u
        packed = publish(0, x, w * scale, packed)
    zp[0] = packed
    halo_sent(1)

    def coefficients(first, gamma, delta, gamma_old, alpha_old):
        beta = jnp.where(first, 0.0, gamma / gamma_old)
        return beta, gamma / (delta - beta * gamma / alpha_old)

    def iteration(i, carry):
        gamma_old, alpha_old, row = carry
        par = lax.rem(i, 2)
        later = 1 - par
        sum_start(par, 0, row)
        halo_start(par)
        stencil_local(par)
        gradient_prepare(i)
        for phase in range(1, len(PHASES)):
            sum_start(par, phase, sum_wait(par, phase - 1))
        gradient_send(i)
        halo_wait(par)
        zc = z_correction(par)
        for x in range(lx):
            nb[x] = corrected(par, x, zc)
        gamma, delta = unpair(sum_wait(par, len(PHASES) - 1))
        beta, alpha = coefficients(i == 0, gamma, delta, gamma_old, alpha_old)
        packed = jnp.zeros((ly, lz), F32)
        gamma_sum = jnp.zeros((ly, lz), F32)
        delta_sum = jnp.zeros((ly, lz), F32)
        for x in range(lx):
            r, w, scale = resid[x], wv[x], inv[x]
            z = (w - nb[x]) + beta * zv[x]
            s = w + beta * sv[x]
            p = r * scale + beta * pv[x]
            zv[x] = z
            sv[x] = s
            pv[x] = p
            press[x] = press[x] + alpha * p
            r = r - alpha * s
            w = w - alpha * z
            resid[x] = r
            wv[x] = w
            u = r * scale
            gamma_sum = gamma_sum + r * u
            delta_sum = delta_sum + w * u
            packed = publish(later, x, w * scale, packed)
        zp[later] = packed
        halo_sent(par)
        sums_sent(par)
        return gamma, alpha, pair_row(gamma_sum, delta_sum)

    ones = jnp.ones((1, lz), F32)
    gamma_old, alpha_old, row = lax.fori_loop(
        0, ITERS - 1, iteration, (ones, ones, pair_row(gamma, delta))
    )
    par = (ITERS - 1) % 2
    sum_start(par, 0, row)
    gradient_finish()
    for phase in range(1, len(PHASES)):
        sum_start(par, phase, sum_wait(par, phase - 1))
    gamma, delta = unpair(sum_wait(par, len(PHASES) - 1))
    beta, alpha = coefficients(ITERS == 1, gamma, delta, gamma_old, alpha_old)
    for x in range(lx):
        r = resid[x]
        s = wv[x] + beta * sv[x]
        p = r * inv[x] + beta * pv[x]
        press[x] = press[x] + alpha * p
        resid[x] = r - alpha * s
    sums_sent(par)


def pressure_solve(right_side, diagonal, feats, w1, w2, w3, grads):
    sizes = {a: lax.axis_size(a) for a in AXES}
    lx, ly, lz = right_side.shape
    slots = 0
    for axes in PHASES:
        n = 1
        for a in axes:
            n *= sizes[a]
        slots += n
    nx, nz, na = (sizes[a] for a in ("gx", "gz", "ga"))
    rows, ch = grads.shape
    share = rows // nz
    piece = share // na
    copies = max(2 * (nz - 1) + 2 * (na - 1) + nx - 1, 1)
    field = pltpu.VMEM((lx, ly, lz), F32)
    vmem = pl.BlockSpec(memory_space=pltpu.VMEM)
    return pl.pallas_call(
        functools.partial(solve_kernel, sizes),
        out_shape=[jax.ShapeDtypeStruct((lx, ly, lz), F32)] * 2
        + [jax.ShapeDtypeStruct(w.shape, F32) for w in (w1, w2, w3)],
        in_specs=[vmem] * 7,
        out_specs=[vmem] * 5,
        scratch_shapes=[
            pltpu.VMEM((2, lx + 8, ly + 16, lz), F32),
            field, field, field, field, field, field,
            pltpu.VMEM((2, lx, 8, lz), F32),
            pltpu.VMEM((2, 2, lx, 8, lz), F32),
            pltpu.VMEM((2, ly, lz), F32),
            pltpu.VMEM((2, 2, ly, lz), F32),
            pltpu.VMEM((2, len(PHASES), 1, lz), F32),
            pltpu.VMEM((2, slots, 1, lz), F32),
            pltpu.VMEM((max(nz - 1, 1), share, ch), F32),
            pltpu.VMEM((share, ch), F32),
            pltpu.VMEM((max(na - 1, 1), piece, ch), F32),
            pltpu.VMEM((piece, ch), F32),
            pltpu.VMEM((nx, piece, ch), F32),
            pltpu.VMEM((rows, ch), F32),
            pltpu.SemaphoreType.DMA((copies,)),
            pltpu.SemaphoreType.DMA((copies,)),
            pltpu.SemaphoreType.DMA((6,)),
            pltpu.SemaphoreType.DMA((2, 6)),
            pltpu.SemaphoreType.DMA((slots,)),
            pltpu.SemaphoreType.DMA((2, slots)),
        ],
        compiler_params=pltpu.CompilerParams(collective_id=0, has_side_effects=True),
        cost_estimate=pl.CostEstimate(
            flops=60_000_000, bytes_accessed=200_000_000, transcendentals=0
        ),
    )(right_side, diagonal, feats, w1, w2, w3, grads)


def body(
    right_side, diagonal, element_features, sample_bank, target_bank, patch_index, w_first, w_second, w_third
):
    unit = 8 * lax.axis_size("gz") * lax.axis_size("ga")
    rows = w_first.shape[0] + w_second.shape[0] + w_third.shape[0]
    rows = (rows + unit - 1) // unit * unit
    grads = closure_gradients(
        sample_bank, target_bank, patch_index, w_first, w_second, w_third, rows
    )
    return tuple(
        pressure_solve(
            right_side, diagonal, element_features, w_first, w_second, w_third, grads
        )
    )


def solution(mesh):
    return jax.shard_map(
        body,
        mesh=mesh,
        in_specs=(
            P("gx", "ga", "gz"),
            P("gx", "ga", "gz"),
            P(None, ("gx", "gz", "ga")),
            P(None, ("gx", "gz", "ga")),
            P(None, ("gx", "gz", "ga")),
            P(("gx", "gz", "ga")),
            P(),
            P(),
            P(),
        ),
        out_specs=(P("gx", "ga", "gz"), P("gx", "ga", "gz"), P(), P(), P()),
        check_vma=False,
    )
```

profile of v0, /device:TPU:1, one launch (start us, length us, event | category | flops | bytes accessed | tf_op | source)
XLA Modules:
  0.0 116.6 jit_solution(1916504011279470385)
XLA Ops:
  0.6 13.6 %shard_map.128.grads = f32[640,256]{1,0:T(8,128)} custom-call(bf16[256,4096]{1,0:T(8,128)(2,1)} %bank.1, bf16[6,4096]{1,0:T(8,128)(2,1)} %target.1, s32[1,2048]{1,0:T(1,128)} %bitcast.1, bf16[256,256]{1,0:T(8,128)(2,1)} %w1.3, bf16[256,256]{1,0:T(8,128)(2,1)} %w2.3, bf16[6,256]{1,0:T(8,128)(2,1)} %w3.3), custom_call_target="tpu_custom_call" | custom-call | flops 3758096384 | bytes 2097152 | tf_op jit(solution)/shard_map/pallas_call | solution.py:81
  14.2 95.1 %shard_map.129 = (f32[16,32,128]{2,1,0:T(8,128)}, f32[16,32,128]{2,1,0:T(8,128)}, f32[256,256]{1,0:T(8,128)}, f32[256,256]{1,0:T(8,128)}, f32[6,256]{1,0:T(8,128)}) custom-call(f32[16,32,128]{2,1,0:T(8,128)} %right.1, f32[16,32,128]{2,1,0:T(8,128)} %diag.1, bf16[256,128]{1,0:T(8,128)(2,1)} %feats.1, bf16[256,256]{1,0:T(8,128)(2,1)} %w1.3, ...), custom_call_target="tpu_custom_call" | custom-call | flops 60000000 | bytes 200000000 | tf_op jit(solution)/shard_map/pallas_call | solution.py:560
  109.3 0.0 copy-start
  109.3 1.7 %copy.19 = f32[16,32,128]{2,1,0:T(8,128)} copy(f32[16,32,128]{2,1,0:T(8,128)} %get-tuple-element.10) | data formatting | bytes 524288
  111.0 1.7 %copy.20 = f32[16,32,128]{2,1,0:T(8,128)} copy(f32[16,32,128]{2,1,0:T(8,128)} %get-tuple-element.11) | data formatting | bytes 524288
  112.7 1.7 %copy.21 = f32[256,256]{1,0:T(8,128)} copy(f32[256,256]{1,0:T(8,128)} %get-tuple-element.12) | data formatting | bytes 524288
  114.3 1.7 %copy.22 = f32[256,256]{1,0:T(8,128)} copy(f32[256,256]{1,0:T(8,128)} %get-tuple-element.13) | data formatting | bytes 524288
  116.0 0.0 copy-done
  116.0 0.6 copy.23
Async XLA Ops:
  109.3 6.7 %copy-start = (f32[6,256]{1,0:T(8,128)S(1)}, f32[6,256]{1,0:T(8,128)}, u32[]{:S(2)}) copy-start(f32[6,256]{1,0:T(8,128)} %get-tuple-element.14) | copy-start | bytes 18436
where the time goes:
time: 118 us; the launch traced here: 117 us
  Pallas kernels  109 us (92%)
  local copies, waits for them, and re-layouts  7.29 us (6%)
    pallas_call x1, Pallas kernels, pressure_solve(): pl.pallas_call(functools.partial(solve_kernel, sizes), out_shape=[jax.Sha...  95.1 us
    pallas_call x1, Pallas kernels, closure_gradients(): pl.pallas_call(grad_kernel, grid=(columns // TILE,), in_specs=[pl.BlockSp...  13.6 us
    unnamed x7, local copies, waits for them, and re-layouts  7.29 us

commit v1 on v0

v1 whole, which is shorter than its diff:
```python
import functools

import jax
import jax.numpy as jnp
from jax import lax
from jax.experimental import pallas as pl
from jax.experimental.pallas import tpu as pltpu
from jax.sharding import PartitionSpec as P

EL = 8
ITERS = 12
TILE = 512
AXES = ("gx", "gz", "ga")
ONE_PHASE = 64

taps = (1.6, -0.2, 8.0 / 315.0, -1.0 / 560.0)
center = 3.0 * 205.0 / 72.0
epsilon = 1e-06
half = 1.1
MESH = pl.DeviceIdType.MESH
F32 = jnp.float32
BF16 = jnp.bfloat16


def dot(a, b, dims=((1,), (0,)), precision=None):
    return lax.dot_general(a, b, (dims, ((), ())), preferred_element_type=F32, precision=precision)


def sigmoid(v):
    return 1.0 / (1.0 + jnp.exp(-v))


def phases_of(sizes):
    total = 1
    for a in AXES:
        total *= sizes[a]
    return (AXES,) if total <= ONE_PHASE else (("gx",), ("gz", "ga"))


def shift_offsets(sizes):
    combos = [()]
    for n in sizes:
        combos = [c + (k,) for c in combos for k in range(n)]
    return combos[1:]


def krylov_coefficients(mu):
    n = len(mu) // 2
    one = jnp.ones_like(mu[0])
    rho, pi = dict(enumerate(mu)), dict(enumerate(mu))
    r, p, x = [one], [one], []
    for k in range(n):
        last = 2 * n - 2 - k
        tau = {}
        for l in range(k, last + 1):
            tau[l] = pi[l] + 0.5 * (pi[l + 1] + pi[abs(l - 1)])
        alpha = rho[k] / tau[k]
        x = [a + alpha * b for a, b in zip(x, p)] + [alpha * b for b in p[len(x):]]
        moved = list(p) + [jnp.zeros_like(one)]
        for j, b in enumerate(p):
            if j == 0:
                moved[1] = moved[1] + b
            else:
                moved[j - 1] = moved[j - 1] + 0.5 * b
                moved[j + 1] = moved[j + 1] + 0.5 * b
        r = [a - alpha * b for a, b in zip(r + [jnp.zeros_like(one)], moved)]
        if k + 1 < n:
            new = {l: rho[l] - alpha * tau[l] for l in range(k + 1, last + 1)}
            beta = (-alpha if k == 0 else -0.5 * alpha) * new[k + 1] / rho[k]
            p = [a + beta * b for a, b in zip(r, p)] + r[len(p):]
            pi = {l: (new[l] if l > k else 0.0) + beta * pi[l] for l in range(k, last + 1)}
            rho = new
    return [v * (1.0 / half) for v in x], r


def solve_kernel(
    sizes, right, diag, feats, bank, target, index, w1, w2, w3, press, resid, total_grads,
    mp, nb, basis, pre, inv, yp, yr, zp, zr, eta, ar_src, ar_dst,
    bank_v, counts, grads, first, held, second, owned, third, full,
    bank_sem, g_send, g_recv, h_send, h_recv, a_send, a_recv,
):
    lx, ly, lz = right.shape
    ch, columns = bank.shape
    stress = target.shape[0]
    tiles = columns // TILE
    pos = {a: lax.axis_index(a) for a in AXES}
    phases = phases_of(sizes)

    def tile_copy(t):
        return pltpu.make_async_copy(
            bank.at[:, pl.ds(t * TILE, TILE)], bank_v.at[t], bank_sem.at[t]
        )

    for t in range(tiles):
        tile_copy(t).start()

    def coords(axes, offs, sign):
        out = {}
        for a, k in zip(axes, offs):
            n = sizes[a]
            c = pos[a] + (k if sign > 0 else n - k) if k else pos[a]
            out[a] = lax.rem(c, n) if k else c
        return out

    def flat(axes, at):
        value = 0
        for a in axes:
            value = value * sizes[a] + at[a]
        return value

    groups = []
    for axes in phases:
        me = flat(axes, pos)
        peers = []
        for offs in shift_offsets([sizes[a] for a in axes]):
            to = {**pos, **coords(axes, offs, 1)}
            source = flat(axes, coords(axes, offs, -1))
            peers.append((to, source))
        groups.append((me, peers))

    nx, nz, na = sizes["gx"], sizes["gz"], sizes["ga"]
    share = grads.shape[0] // nz
    piece = share // na

    def block_of(iz, ia=None):
        if ia is None:
            return pl.ds(pl.multiple_of(iz * share, 8), share)
        return pl.ds(pl.multiple_of((iz * na + ia) * piece, 8), piece)

    def along(axis, k, sign):
        return coords((axis,), (k,), sign)[axis]

    def gather_copy(number, axis, k, src, dst):
        return pltpu.make_async_remote_copy(
            src_ref=src,
            dst_ref=dst,
            send_sem=g_send.at[number],
            recv_sem=g_recv.at[number],
            device_id={**pos, axis: along(axis, k, 1)},
            device_id_type=MESH,
        )

    def scatter_gz(k):
        return gather_copy(k - 1, "gz", k, grads.at[block_of(along("gz", k, 1))], first.at[k - 1])

    def scatter_ga(k):
        rows = pl.ds(pl.multiple_of(along("ga", k, 1) * piece, 8), piece)
        return gather_copy(nz - 1 + k - 1, "ga", k, held.at[rows], second.at[k - 1])

    def add_gx(k, sign=1):
        slot = pos["gx"] if sign > 0 else along("gx", k, -1)
        return gather_copy(nz + na - 2 + k - 1, "gx", k, owned, third.at[slot])

    def gather_ga(k, sign=1):
        at = pos["ga"] if sign > 0 else along("ga", k, -1)
        rows = block_of(pos["gz"], at)
        return gather_copy(nz + na + nx - 3 + k - 1, "ga", k, full.at[rows], full.at[rows])

    def gather_gz(k, sign=1):
        at = pos["gz"] if sign > 0 else along("gz", k, -1)
        rows = block_of(at)
        return gather_copy(nz + 2 * na + nx - 4 + k - 1, "gz", k, full.at[rows], full.at[rows])

    def gradient_stage(stage):
        if stage == 0:
            for k in range(1, nz):
                scatter_gz(k).start()
        elif stage == 1:
            total = grads[block_of(pos["gz"]), :]
            for k in range(1, nz):
                scatter_gz(k).wait_recv()
                total = total + first[k - 1]
            held[...] = total
            for k in range(1, na):
                scatter_ga(k).start()
        elif stage == 2:
            total = held[pl.ds(pl.multiple_of(pos["ga"] * piece, 8), piece), :]
            for k in range(1, na):
                scatter_ga(k).wait_recv()
                total = total + second[k - 1]
            owned[...] = total
            third[pos["gx"]] = total
            for k in range(1, nx):
                add_gx(k).start()
        elif stage == 3:
            for k in range(1, nx):
                add_gx(k, -1).wait_recv()
            full[block_of(pos["gz"], pos["ga"]), :] = jnp.sum(third[...], axis=0)
            for k in range(1, na):
                gather_ga(k).start()
        elif stage == 4:
            for k in range(1, na):
                gather_ga(k, -1).wait_recv()
            for k in range(1, nz):
                gather_gz(k).start()
        else:
            for k in range(1, nz):
                gather_gz(k, -1).wait_recv()
                scatter_gz(k).wait_send()
                gather_gz(k).wait_send()
            for k in range(1, na):
                scatter_ga(k).wait_send()
                gather_ga(k).wait_send()
            for k in range(1, nx):
                add_gx(k).wait_send()

    def count_samples():
        samples = index.shape[1]
        ids = index[...]
        high = lax.broadcasted_iota(jnp.int32, (columns // 128, samples), 0) == (ids // 128)
        low = lax.broadcasted_iota(jnp.int32, (128, samples), 0) == (ids % 128)
        counts[...] = dot(
            jnp.where(high, 1.0, 0.0).astype(BF16),
            jnp.where(low, 1.0, 0.0).astype(BF16),
            ((1,), (1,)),
        )

    def gradient_tile(t):
        rows = TILE // 128
        tile_copy(t).wait()
        weight = jnp.concatenate([counts[pl.ds(t * rows + j, 1), :] for j in range(rows)], axis=1)
        x = bank_v[t]
        a1, a2, a3 = w1[...], w2[...], w3[...]
        l1 = dot(a1, x)
        s1 = sigmoid(l1)
        h1 = (l1 * s1).astype(BF16)
        l2 = dot(a2, h1)
        s2 = sigmoid(l2)
        h2 = (l2 * s2).astype(BF16)
        goal = target[:, pl.ds(pl.multiple_of(t * TILE, TILE), TILE)]
        error = (dot(a3, h2) - goal.astype(F32)).astype(BF16)

        def weighted(delta, right):
            scaled = delta.astype(F32) * weight
            upper = scaled.astype(BF16)
            lower = (scaled - upper.astype(F32)).astype(BF16)
            return dot(upper, right, ((1,), (1,))) + dot(lower, right, ((1,), (1,)))

        grads[2 * ch : 2 * ch + stress] += weighted(error, h2)
        d2 = (dot(a3, error, ((0,), (0,))) * (s2 * (1.0 + l2 * (1.0 - s2)))).astype(BF16)
        grads[ch : 2 * ch] += weighted(d2, h1)
        d1 = (dot(a2, d2, ((0,), (0,))) * (s1 * (1.0 + l1 * (1.0 - s1)))).astype(BF16)
        grads[:ch] += weighted(d1, x)

    def gradient_work(i):
        pl.when(i < tiles)(lambda: gradient_tile(i))
        for stage in range(ITERS - tiles):
            pl.when(i == tiles + stage)(lambda stage=stage: gradient_stage(stage))

    mp[...] = jnp.zeros_like(mp)
    yr[...] = jnp.zeros_like(yr)
    zr[...] = jnp.zeros_like(zr)

    barrier = pltpu.get_barrier_semaphore()
    total = 0
    for _, peers in groups:
        for to, _ in peers:
            pl.semaphore_signal(barrier, inc=1, device_id=to, device_id_type=MESH)
            total += 1

    lane = lax.broadcasted_iota(jnp.int32, (ly, lz), 1)
    sub8 = lax.broadcasted_iota(jnp.int32, (8, lz), 0)

    def halo_copies(par):
        out = {}

        def add(axis, step, number, src, dst):
            copy = pltpu.make_async_remote_copy(
                src_ref=src,
                dst_ref=dst,
                send_sem=h_send.at[par, number],
                recv_sem=h_recv.at[par, number],
                device_id={**pos, axis: jnp.clip(pos[axis] + step, 0, sizes[axis] - 1)},
                device_id_type=MESH,
            )
            can_send = pos[axis] < sizes[axis] - 1 if step > 0 else pos[axis] > 0
            will_get = pos[axis] > 0 if step > 0 else pos[axis] < sizes[axis] - 1
            out.setdefault(axis, []).append((copy, can_send, will_get))

        rows = pl.ds(8, ly)
        if sizes["gx"] > 1:
            add("gx", 1, 0, mp.at[par, pl.ds(lx, 4), rows], mp.at[par, pl.ds(0, 4), rows])
            add("gx", -1, 1, mp.at[par, pl.ds(4, 4), rows], mp.at[par, pl.ds(lx + 4, 4), rows])
        if sizes["ga"] > 1:
            add("ga", 1, 2, yp.at[par, 0], yr.at[par, 0])
            add("ga", -1, 3, yp.at[par, 1], yr.at[par, 1])
        if sizes["gz"] > 1:
            add("gz", 1, 4, zp.at[par], zr.at[par, 0])
            add("gz", -1, 5, zp.at[par], zr.at[par, 1])
        return out

    def halo_start(par, *axes):
        copies = halo_copies(par)
        for axis in axes:
            for copy, can_send, _ in copies.get(axis, []):
                pl.when(can_send)(copy.start)

    def halo_wait(par):
        for copies in halo_copies(par).values():
            for copy, _, will_get in copies:
                pl.when(will_get)(copy.wait_recv)

    def halo_sent(par):
        for copies in halo_copies(par).values():
            for copy, can_send, _ in copies:
                pl.when(can_send)(copy.wait_send)

    bases = []
    base = 0
    for axes in phases:
        bases.append(base)
        n = 1
        for a in axes:
            n *= sizes[a]
        base += n

    def sum_copies(phase):
        me, peers = groups[phase]
        out = []
        for k, (to, source) in enumerate(peers):
            slot = bases[phase]
            send = pltpu.make_async_remote_copy(
                src_ref=ar_src.at[phase],
                dst_ref=ar_dst.at[slot + me],
                send_sem=a_send.at[slot + k],
                recv_sem=a_recv.at[slot + me],
                device_id=to,
                device_id_type=MESH,
            )
            receive = pltpu.make_async_remote_copy(
                src_ref=ar_src.at[phase],
                dst_ref=ar_dst.at[slot + source],
                send_sem=a_send.at[slot + k],
                recv_sem=a_recv.at[slot + source],
                device_id=to,
                device_id_type=MESH,
            )
            out.append((send, receive))
        return out

    def sum_start(phase, row):
        ar_src[phase] = row
        ar_dst[bases[phase] + groups[phase][0]] = row
        for send, _ in sum_copies(phase):
            send.start()

    def sum_wait(phase):
        count = len(groups[phase][1]) + 1
        for _, receive in sum_copies(phase):
            receive.wait_recv()
        return jnp.sum(ar_dst[pl.ds(bases[phase], count)], axis=0)

    def sums_sent():
        for phase in range(len(phases)):
            for send, _ in sum_copies(phase):
                send.wait_send()

    def stencil_local(par):
        for x in range(lx):
            v = mp[par, 4 + x, pl.ds(8, ly)]
            acc = None
            for k in range(1, 5):
                t = mp[par, 4 + x, pl.ds(8 + k, ly)] + mp[par, 4 + x, pl.ds(8 - k, ly)]
                if x + k < lx:
                    t = t + mp[par, 4 + x + k, pl.ds(8, ly)]
                if x - k >= 0:
                    t = t + mp[par, 4 + x - k, pl.ds(8, ly)]
                t = t + jnp.where(lane >= k, pltpu.roll(v, k, 1), 0.0)
                t = t + jnp.where(lane < lz - k, pltpu.roll(v, lz - k, 1), 0.0)
                t = taps[k - 1] * t
                acc = t if acc is None else acc + t
            nb[x] = acc

    def z_correction(par):
        h = jnp.where(lane % 8 < 4, zr[par, 0], zr[par, 1])
        acc = jnp.zeros((ly, lz), F32)
        place = lane % 8
        for k in range(1, 5):
            ahead = jnp.where((place >= 4) & (place - 4 < k), pltpu.roll(h, k, 1), 0.0)
            behind = jnp.where((place < 4) & (place >= 4 - k), pltpu.roll(h, lz - k, 1), 0.0)
            acc = acc + taps[k - 1] * (ahead + behind)
        return acc

    def corrected(par, x, zc):
        acc = nb[x]
        for k in range(1, 5):
            if x - k < 0:
                acc = acc + taps[k - 1] * mp[par, 4 + x - k, pl.ds(8, ly)]
            if x + k >= lx:
                acc = acc + taps[k - 1] * mp[par, 4 + x + k, pl.ds(8, ly)]
        z = pltpu.roll(zc, (2 * lz - 8 * x - 4) % lz, 1)
        acc = acc + jnp.where((lane < 4) | (lane >= lz - 4), z, 0.0)
        if x % 2 == 0:
            h = jnp.where(sub8 < 4, yr[par, 1, x // 2], yr[par, 0, x // 2])
        else:
            h = pltpu.roll(jnp.where(sub8 < 4, yr[par, 0, x // 2], yr[par, 1, x // 2]), 4, 0)
        low = jnp.zeros((8, lz), F32)
        high = jnp.zeros((8, lz), F32)
        for k in range(1, 5):
            low = low + taps[k - 1] * jnp.where(sub8 < k, pltpu.roll(h, k, 0), 0.0)
            high = high + taps[k - 1] * jnp.where(sub8 >= 8 - k, pltpu.roll(h, 8 - k, 0), 0.0)
        parts = [acc[:8] + low] + ([acc[8:-8]] if ly > 16 else []) + [acc[-8:] + high]
        return jnp.concatenate(parts, axis=0)

    def publish(par, x, m, packed, edges):
        mp[par, 4 + x, pl.ds(8, ly)] = m
        if x % 2 == 0:
            edges = (m[:8], m[-8:])
        else:
            yp[par, 0, x // 2] = jnp.where(sub8 < 4, pltpu.roll(m[-8:], 4, 0), edges[1])
            yp[par, 1, x // 2] = jnp.where(sub8 < 4, edges[0], pltpu.roll(m[:8], 4, 0))
        turned = pltpu.roll(m, (8 * x + 4) % lz, 1)
        return jnp.where((lane >= 8 * x) & (lane < 8 * x + 8), turned, packed), edges

    order = list(range(4)) + list(range(lx - 4, lx)) + list(range(4, lx - 4))

    hidden = dot(w1[...], feats[...])
    hidden = (hidden * sigmoid(hidden)).astype(BF16)
    hidden = dot(w2[...], hidden)
    hidden = (hidden * sigmoid(hidden)).astype(BF16)
    predicted = dot(w3[...], hidden)
    trace = (predicted[0:1] + predicted[1:2] + predicted[2:3]) / 3.0
    ex, ey, ez = lx // EL, ly // EL, lz // EL
    spread = jnp.where(
        lax.broadcasted_iota(jnp.int32, (lz, lz), 0) == lax.broadcasted_iota(jnp.int32, (lz, lz), 1) // EL,
        1.0,
        0.0,
    )
    lines = jnp.concatenate(
        [trace if e == 0 else pltpu.roll(trace, (lz - e * ez) % lz, 1) for e in range(ex * ey)], axis=0
    )
    forcing = dot(lines, spread, precision=lax.Precision.HIGHEST)
    pl.semaphore_wait(barrier, total)
    packed = jnp.zeros((ly, lz), F32)
    edges = None
    for n, x in enumerate(order):
        line = forcing[(x // EL) * ey : (x // EL) * ey + ey]
        block = jnp.concatenate([jnp.broadcast_to(line[j : j + 1], (EL, lz)) for j in range(ey)], axis=0)
        whole = diag[x] + center
        scale = 1.0 / whole
        pre[x] = whole
        inv[x] = scale * (2.0 / half)
        first_vector = (right[x] + block) * scale
        basis[0, x] = first_vector
        packed, edges = publish(0, x, first_vector, packed, edges)
        if n == 7:
            halo_start(0, "gx")
    zp[0] = packed
    halo_start(0, "ga", "gz")
    grads[...] = jnp.zeros_like(grads)
    count_samples()

    def iteration(i, carry):
        par = lax.rem(i, 2)
        later = 1 - par
        stencil_local(par)
        gradient_work(i)
        halo_wait(par)
        zc = z_correction(par)
        start = jnp.where(i == 0, 0.5, 1.0)
        back = jnp.where(i == 0, 0.0, 1.0)
        keep = start * (2.0 / half - 2.0)
        more = i < ITERS - 1
        packed = jnp.zeros((ly, lz), F32)
        even = jnp.zeros((ly, lz), F32)
        odd = jnp.zeros((ly, lz), F32)
        edges = None
        older = jnp.maximum(i - 1, 0)
        for n, x in enumerate(order):
            v = mp[par, 4 + x, pl.ds(8, ly)]
            m = keep * v - start * (inv[x] * corrected(par, x, zc)) - back * basis[older, x]
            basis[i + 1, x] = m
            weighed = pre[x] * v
            even = even + weighed * v
            odd = odd + weighed * m
            packed, edges = publish(later, x, m, packed, edges)
            if n == 7:
                pl.when(more)(lambda: halo_start(later, "gx"))
        zp[later] = packed
        pl.when(more)(lambda: halo_start(later, "ga", "gz"))
        eta[2 * i] = jnp.sum(even.reshape(ly // 8, 8, lz), axis=0)
        eta[2 * i + 1] = jnp.sum(odd.reshape(ly // 8, 8, lz), axis=0)
        halo_sent(par)
        return carry

    lax.fori_loop(0, ITERS, iteration, 0)

    count = 2 * ITERS
    sums = jnp.sum(jnp.sum(eta[...], axis=1), axis=1, keepdims=True)
    mine = lax.broadcasted_iota(jnp.int32, (count, lz), 0) == lax.broadcasted_iota(jnp.int32, (count, lz), 1)
    row = jnp.sum(jnp.where(mine, sums, 0.0), axis=0, keepdims=True)
    sum_start(0, row)
    for stage in range(ITERS - tiles, 5):
        gradient_stage(stage)
    for phase in range(1, len(phases)):
        sum_start(phase, sum_wait(phase - 1))
    row = sum_wait(len(phases) - 1)
    spread_row = jnp.sum(jnp.where(mine, row, 0.0), axis=1, keepdims=True)
    moment = [jnp.broadcast_to(spread_row[j : j + 1], (1, lz)) for j in range(count)]
    mu = moment[:2] + [2.0 * moment[j] - moment[j % 2] for j in range(2, count)]
    along_x, along_r = krylov_coefficients(mu)
    for x in range(lx):
        p = along_x[0] * basis[0, x]
        r = along_r[0] * basis[0, x]
        for j in range(1, ITERS):
            v = basis[j, x]
            p = p + along_x[j] * v
            r = r + along_r[j] * v
        press[x] = p
        resid[x] = pre[x] * (r + along_r[ITERS] * basis[ITERS, x])
    gradient_stage(5)
    total_grads[...] = full[...]
    sums_sent()


def pressure_solve(right_side, diagonal, feats, bank, target, index, w1, w2, w3):
    sizes = {a: lax.axis_size(a) for a in AXES}
    lx, ly, lz = right_side.shape
    ch, columns = bank.shape
    slots = 0
    phases = phases_of(sizes)
    for axes in phases:
        n = 1
        for a in axes:
            n *= sizes[a]
        slots += n
    nx, nz, na = (sizes[a] for a in ("gx", "gz", "ga"))
    unit = 8 * nz * na
    rows = w1.shape[0] + w2.shape[0] + w3.shape[0]
    rows = (rows + unit - 1) // unit * unit
    share = rows // nz
    piece = share // na
    tiles = columns // TILE
    copies = max(2 * (nz - 1) + 2 * (na - 1) + nx - 1, 1)
    field = pltpu.VMEM((lx, ly, lz), F32)
    vmem = pl.BlockSpec(memory_space=pltpu.VMEM)
    return pl.pallas_call(
        functools.partial(solve_kernel, sizes),
        out_shape=[jax.ShapeDtypeStruct((lx, ly, lz), F32)] * 2 + [jax.ShapeDtypeStruct((rows, ch), F32)],
        in_specs=[vmem] * 3 + [pl.BlockSpec(memory_space=pl.ANY)] + [vmem] * 5,
        out_specs=[vmem] * 3,
        scratch_shapes=[
            pltpu.VMEM((2, lx + 8, ly + 16, lz), F32),
            field,
            pltpu.VMEM((ITERS + 1, lx, ly, lz), F32),
            field, field,
            pltpu.VMEM((2, 2, lx // 2, 8, lz), F32),
            pltpu.VMEM((2, 2, lx // 2, 8, lz), F32),
            pltpu.VMEM((2, ly, lz), F32),
            pltpu.VMEM((2, 2, ly, lz), F32),
            pltpu.VMEM((2 * ITERS, 8, lz), F32),
            pltpu.VMEM((len(phases), 1, lz), F32),
            pltpu.VMEM((slots, 1, lz), F32),
            pltpu.VMEM((tiles, ch, TILE), BF16),
            pltpu.VMEM((columns // 128, 128), F32),
            pltpu.VMEM((rows, ch), F32),
            pltpu.VMEM((max(nz - 1, 1), share, ch), F32),
            pltpu.VMEM((share, ch), F32),
            pltpu.VMEM((max(na - 1, 1), piece, ch), F32),
            pltpu.VMEM((piece, ch), F32),
            pltpu.VMEM((nx, piece, ch), F32),
            pltpu.VMEM((rows, ch), F32),
            pltpu.SemaphoreType.DMA((tiles,)),
            pltpu.SemaphoreType.DMA((copies,)),
            pltpu.SemaphoreType.DMA((copies,)),
            pltpu.SemaphoreType.DMA((2, 6)),
            pltpu.SemaphoreType.DMA((2, 6)),
            pltpu.SemaphoreType.DMA((slots,)),
            pltpu.SemaphoreType.DMA((slots,)),
        ],
        compiler_params=pltpu.CompilerParams(collective_id=0, has_side_effects=True),
        cost_estimate=pl.CostEstimate(
            flops=60_000_000, bytes_accessed=200_000_000, transcendentals=0
        ),
    )(right_side, diagonal, feats, bank, target, index.reshape(1, -1), w1, w2, w3)


def finish_kernel(press_in, resid_in, grads, press, resid, step1, step2, step3):
    press[...] = press_in[...]
    resid[...] = resid_in[...]
    ch = step1.shape[0]
    start = 0
    for out in (step1, step2, step3):
        count = out.shape[0]
        value = grads[start : start + count]
        squares = jnp.sum(jnp.sum(value * value, axis=0, keepdims=True), axis=1, keepdims=True)
        out[...] = value * lax.rsqrt(squares / (count * ch) + epsilon)
        start += count


def finish(press, resid, grads, weights):
    vmem = pl.BlockSpec(memory_space=pltpu.VMEM)
    return pl.pallas_call(
        finish_kernel,
        out_shape=[jax.ShapeDtypeStruct(press.shape, F32)] * 2
        + [jax.ShapeDtypeStruct(w.shape, F32) for w in weights],
        in_specs=[vmem] * 3,
        out_specs=[vmem] * 5,
        cost_estimate=pl.CostEstimate(flops=1_000_000, bytes_accessed=2_000_000, transcendentals=0),
    )(press, resid, grads)


def body(
    right_side, diagonal, element_features, sample_bank, target_bank, patch_index, w_first, w_second, w_third
):
    weights = (w_first, w_second, w_third)
    solved = pressure_solve(
        right_side, diagonal, element_features, sample_bank, target_bank, patch_index, *weights
    )
    return tuple(finish(*solved, weights))


def solution(mesh):
    return jax.shard_map(
        body,
        mesh=mesh,
        in_specs=(
            P("gx", "ga", "gz"),
            P("gx", "ga", "gz"),
            P(None, ("gx", "gz", "ga")),
            P(None, ("gx", "gz", "ga")),
            P(None, ("gx", "gz", "ga")),
            P(("gx", "gz", "ga")),
            P(),
            P(),
            P(),
        ),
        out_specs=(P("gx", "ga", "gz"), P("gx", "ga", "gz"), P(), P(), P()),
        check_vma=False,
    )
```

time: 118 us -> 70.4 us (0.60); the launches traced: 117 us -> 70.2 us
  Pallas kernels: 109 us -> 69.6 us
  local copies, waits for them, and re-layouts: 7.29 us -> 0 us
    pallas_call x1, Pallas kernels: 95.1 us -> 67.3 us  [pressure_solve(): pl.pallas_call(functools.partial(solve_kernel, sizes), out_shape=[jax.Sha...]
    pallas_call x1, Pallas kernels: 13.6 us -> 2.28 us  [finish(): pl.pallas_call(finish_kernel, out_shape=[jax.ShapeDtypeStruct(press.shape...]
    unnamed x7 -> x0, local copies, waits for them, and re-layouts: 7.29 us -> none
where the time goes in v1:
time: 70.4 us; the launch traced here: 70.2 us
  Pallas kernels  69.6 us (99%)
    pallas_call x1, Pallas kernels, pressure_solve(): pl.pallas_call(functools.partial(solve_kernel, sizes), out_shape=[jax.Sha...  67.3 us
    pallas_call x1, Pallas kernels, finish(): pl.pallas_call(finish_kernel, out_shape=[jax.ShapeDtypeStruct(press.shape...  2.28 us

profile of v1, /device:TPU:1, one launch (start us, length us, event | category | flops | bytes accessed | tf_op | source)
XLA Modules:
  0.0 70.2 jit_solution(2695315510095656619)
XLA Ops:
  0.6 67.3 %shard_map.128 = (f32[16,32,128]{2,1,0:T(8,128)}, f32[16,32,128]{2,1,0:T(8,128)}, f32[640,256]{1,0:T(8,128)}) custom-call(f32[16,32,128]{2,1,0:T(8,128)} %right.1, f32[16,32,128]{2,1,0:T(8,128)} %diag.1, bf16[256,128]{1,0:T(8,128)(2,1)} %feats.1, bf16[256,4096]{1,0:T(8,128)(2,1)} %bank.1, bf16[6,4096]{1,0:T(8,128)(2,1)} %target.1, s32[1,2048]{1,0:T(1,128)} %bitcast.1, ...), custom_call_target="tpu_custom_call" | custom-call | flops 60000000 | bytes 200000000 | tf_op jit(solution)/shard_map/pallas_call | solution.py:537
  67.9 2.3 %shard_map.129 = (f32[16,32,128]{2,1,0:T(8,128)}, f32[16,32,128]{2,1,0:T(8,128)}, f32[256,256]{1,0:T(8,128)}, f32[256,256]{1,0:T(8,128)}, f32[6,256]{1,0:T(8,128)}) custom-call(f32[16,32,128]{2,1,0:T(8,128)} %get-tuple-element.8.press_in, f32[16,32,128]{2,1,0:T(8,128)} %get-tuple-element.9.resid_in, f32[640,256]{1,0:T(8,128)} %get-tuple-element.10.grads), custom_call_target="tpu_custom_call" | custom-call | flops 1000000 | bytes 2000000 | tf_op jit(solution)/shard_map/pallas_call | solution.py:593

commit v2 on v1

--- a/solution.py
+++ b/solution.py
@@ -9,9 +9,11 @@
 
 EL = 8
 ITERS = 12
-TILE = 512
+TILE = 256
+TILES_AT_ONCE = 3
 AXES = ("gx", "gz", "ga")
 ONE_PHASE = 64
+STAGES = 7
 
 taps = (1.6, -0.2, 8.0 / 315.0, -1.0 / 560.0)
 center = 3.0 * 205.0 / 72.0
@@ -76,7 +78,8 @@
 def solve_kernel(
     sizes, right, diag, feats, bank, target, index, w1, w2, w3, press, resid, total_grads,
     mp, nb, basis, pre, inv, yp, yr, zp, zr, eta, ar_src, ar_dst,
-    bank_v, counts, grads, first, held, second, owned, third, full,
+    bank_v, counts, grads, swapped, halved, first, held, second, owned, third, full,
+    small, small_in, small_third,
     bank_sem, g_send, g_recv, h_send, h_recv, a_send, a_recv,
 ):
     lx, ly, lz = right.shape
@@ -119,90 +122,163 @@
         groups.append((me, peers))
 
     nx, nz, na = sizes["gx"], sizes["gz"], sizes["ga"]
-    share = grads.shape[0] // nz
+    pair = 2 if nz % 2 == 0 else 1
+    nh = nz // pair
+    side, spot = lax.rem(pos["gz"], pair), lax.div(pos["gz"], pair)
+    half_rows = grads.shape[0] // pair
+    share = half_rows // nh
     piece = share // na
 
-    def block_of(iz, ia=None):
+    def half_of(b):
+        return pl.ds(pl.multiple_of(b * half_rows, 8), half_rows)
+
+    def share_of(h):
+        return pl.ds(pl.multiple_of(h * share, 8), share)
+
+    def block_of(h, ia=None):
+        start = side * half_rows + h * share
         if ia is None:
-            return pl.ds(pl.multiple_of(iz * share, 8), share)
-        return pl.ds(pl.multiple_of((iz * na + ia) * piece, 8), piece)
+            return pl.ds(pl.multiple_of(start, 8), share)
+        return pl.ds(pl.multiple_of(start + ia * piece, 8), piece)
 
     def along(axis, k, sign):
         return coords((axis,), (k,), sign)[axis]
 
-    def gather_copy(number, axis, k, src, dst):
+    def spot_along(k, sign):
+        return lax.rem(spot + (k if sign > 0 else nh - k), nh)
+
+    numbers = {}
+
+    def gradient_copy(kind, k, src, dst, to):
+        number = numbers.setdefault((kind, k), len(numbers))
         return pltpu.make_async_remote_copy(
             src_ref=src,
             dst_ref=dst,
             send_sem=g_send.at[number],
             recv_sem=g_recv.at[number],
-            device_id={**pos, axis: along(axis, k, 1)},
+            device_id={**pos, **to},
             device_id_type=MESH,
         )
 
+    def to_pair():
+        return {"gz": spot * pair + (pair - 1 - side)}
+
+    def to_spot(k):
+        return {"gz": spot_along(k, 1) * pair + side}
+
+    def swap_pair():
+        other = half_of(pair - 1 - side)
+        return [
+            gradient_copy("swap", 0, grads.at[other], swapped, to_pair()),
+            gradient_copy("swap", 1, small.at[0], small_in.at[0], to_pair()),
+        ]
+
     def scatter_gz(k):
-        return gather_copy(k - 1, "gz", k, grads.at[block_of(along("gz", k, 1))], first.at[k - 1])
+        return [
+            gradient_copy("gz", k, halved.at[share_of(spot_along(k, 1))], first.at[k - 1], to_spot(k)),
+            gradient_copy("small gz", k, small.at[1], small_in.at[k], to_spot(k)),
+        ]
 
     def scatter_ga(k):
         rows = pl.ds(pl.multiple_of(along("ga", k, 1) * piece, 8), piece)
-        return gather_copy(nz - 1 + k - 1, "ga", k, held.at[rows], second.at[k - 1])
+        to = {"ga": along("ga", k, 1)}
+        return [
+            gradient_copy("ga", k, held.at[rows], second.at[k - 1], to),
+            gradient_copy("small ga", k, small.at[2], small_in.at[nh + k - 1], to),
+        ]
 
     def add_gx(k, sign=1):
         slot = pos["gx"] if sign > 0 else along("gx", k, -1)
-        return gather_copy(nz + na - 2 + k - 1, "gx", k, owned, third.at[slot])
+        to = {"gx": along("gx", k, 1)}
+        return [
+            gradient_copy("gx", k, owned, third.at[slot], to),
+            gradient_copy("small gx", k, small.at[3], small_third.at[slot], to),
+        ]
 
     def gather_ga(k, sign=1):
         at = pos["ga"] if sign > 0 else along("ga", k, -1)
-        rows = block_of(pos["gz"], at)
-        return gather_copy(nz + na + nx - 3 + k - 1, "ga", k, full.at[rows], full.at[rows])
+        rows = block_of(spot, at)
+        return [gradient_copy("all ga", k, full.at[rows], full.at[rows], {"ga": along("ga", k, 1)})]
 
     def gather_gz(k, sign=1):
-        at = pos["gz"] if sign > 0 else along("gz", k, -1)
-        rows = block_of(at)
-        return gather_copy(nz + 2 * na + nx - 4 + k - 1, "gz", k, full.at[rows], full.at[rows])
+        rows = block_of(spot if sign > 0 else spot_along(k, -1))
+        return [gradient_copy("all gz", k, full.at[rows], full.at[rows], to_spot(k))]
+
+    def gather_pair(sign=1):
+        rows = half_of(side if sign > 0 else pair - 1 - side)
+        return [gradient_copy("all pair", 0, full.at[rows], full.at[rows], to_pair())]
+
+    def start(copies):
+        for copy in copies:
+            copy.start()
+
+    def arrived(copies):
+        for copy in copies:
+            copy.wait_recv()
+
+    def sent(copies):
+        for copy in copies:
+            copy.wait_send()
 
     def gradient_stage(stage):
         if stage == 0:
-            for k in range(1, nz):
-                scatter_gz(k).start()
+            if pair > 1:
+                start(swap_pair())
         elif stage == 1:
-            total = grads[block_of(pos["gz"]), :]
-            for k in range(1, nz):
-                scatter_gz(k).wait_recv()
-                total = total + first[k - 1]
+            total, few = grads[half_of(side), :], small[0]
+            if pair > 1:
+                arrived(swap_pair())
+                total, few = total + swapped[...], few + small_in[0]
+            halved[...] = total
+            small[1] = few
+            for k in range(1, nh):
+                start(scatter_gz(k))
+        elif stage == 2:
+            total, few = halved[share_of(spot), :], small[1]
+            for k in range(1, nh):
+                arrived(scatter_gz(k))
+                total, few = total + first[k - 1], few + small_in[k]
             held[...] = total
+            small[2] = few
             for k in range(1, na):
-                scatter_ga(k).start()
-        elif stage == 2:
-            total = held[pl.ds(pl.multiple_of(pos["ga"] * piece, 8), piece), :]
+                start(scatter_ga(k))
+        elif stage == 3:
+            total, few = held[pl.ds(pl.multiple_of(pos["ga"] * piece, 8), piece), :], small[2]
             for k in range(1, na):
-                scatter_ga(k).wait_recv()
-                total = total + second[k - 1]
+                arrived(scatter_ga(k))
+                total, few = total + second[k - 1], few + small_in[nh + k - 1]
             owned[...] = total
             third[pos["gx"]] = total
+            small[3] = few
+            small_third[pos["gx"]] = few
             for k in range(1, nx):
-                add_gx(k).start()
-        elif stage == 3:
+                start(add_gx(k))
+        elif stage == 4:
             for k in range(1, nx):
-                add_gx(k, -1).wait_recv()
-            full[block_of(pos["gz"], pos["ga"]), :] = jnp.sum(third[...], axis=0)
+                arrived(add_gx(k, -1))
+            full[block_of(spot, pos["ga"]), :] = jnp.sum(third[...], axis=0)
             for k in range(1, na):
-                gather_ga(k).start()
-        elif stage == 4:
+                start(gather_ga(k))
+        elif stage == 5:
             for k in range(1, na):
-                gather_ga(k, -1).wait_recv()
-            for k in range(1, nz):
-                gather_gz(k).start()
+                arrived(gather_ga(k, -1))
+            for k in range(1, nh):
+                start(gather_gz(k))
+        elif stage == 6:
+            for k in range(1, nh):
+                arrived(gather_gz(k, -1))
+            if pair > 1:
+                start(gather_pair())
         else:
-            for k in range(1, nz):
-                gather_gz(k, -1).wait_recv()
-                scatter_gz(k).wait_send()
-                gather_gz(k).wait_send()
+            if pair > 1:
+                arrived(gather_pair(-1))
+                sent(swap_pair() + gather_pair())
+            for k in range(1, nh):
+                sent(scatter_gz(k) + gather_gz(k))
             for k in range(1, na):
-                scatter_ga(k).wait_send()
-                gather_ga(k).wait_send()
+                sent(scatter_ga(k) + gather_ga(k))
             for k in range(1, nx):
-                add_gx(k).wait_send()
+                sent(add_gx(k))
 
     def count_samples():
         samples = index.shape[1]
@@ -236,16 +312,24 @@
             lower = (scaled - upper.astype(F32)).astype(BF16)
             return dot(upper, right, ((1,), (1,))) + dot(lower, right, ((1,), (1,)))
 
-        grads[2 * ch : 2 * ch + stress] += weighted(error, h2)
+        small[0, :stress] += weighted(error, h2)
         d2 = (dot(a3, error, ((0,), (0,))) * (s2 * (1.0 + l2 * (1.0 - s2)))).astype(BF16)
         grads[ch : 2 * ch] += weighted(d2, h1)
         d1 = (dot(a2, d2, ((0,), (0,))) * (s1 * (1.0 + l1 * (1.0 - s1)))).astype(BF16)
         grads[:ch] += weighted(d1, x)
 
+    loops = -(-tiles // TILES_AT_ONCE)
+
     def gradient_work(i):
-        pl.when(i < tiles)(lambda: gradient_tile(i))
-        for stage in range(ITERS - tiles):
-            pl.when(i == tiles + stage)(lambda stage=stage: gradient_stage(stage))
+        def one(t, carry):
+            gradient_tile(t)
+            return carry
+
+        lax.fori_loop(
+            jnp.minimum(i * TILES_AT_ONCE, tiles), jnp.minimum((i + 1) * TILES_AT_ONCE, tiles), one, 0
+        )
+        for stage in range(STAGES):
+            pl.when(i == min(loops - 1 + stage, ITERS - 1))(lambda stage=stage: gradient_stage(stage))
 
     mp[...] = jnp.zeros_like(mp)
     yr[...] = jnp.zeros_like(yr)
@@ -264,7 +348,7 @@
     def halo_copies(par):
         out = {}
 
-        def add(axis, step, number, src, dst):
+        def add(axis, step, number, src, dst, part=None):
             copy = pltpu.make_async_remote_copy(
                 src_ref=src,
                 dst_ref=dst,
@@ -275,12 +359,14 @@
             )
             can_send = pos[axis] < sizes[axis] - 1 if step > 0 else pos[axis] > 0
             will_get = pos[axis] > 0 if step > 0 else pos[axis] < sizes[axis] - 1
-            out.setdefault(axis, []).append((copy, can_send, will_get))
+            out.setdefault(part or axis, []).append((copy, can_send, will_get))
 
         rows = pl.ds(8, ly)
         if sizes["gx"] > 1:
-            add("gx", 1, 0, mp.at[par, pl.ds(lx, 4), rows], mp.at[par, pl.ds(0, 4), rows])
-            add("gx", -1, 1, mp.at[par, pl.ds(4, 4), rows], mp.at[par, pl.ds(lx + 4, 4), rows])
+            add("gx", 1, 0, mp.at[par, pl.ds(lx + 2, 2), rows], mp.at[par, pl.ds(2, 2), rows], "high outer")
+            add("gx", -1, 1, mp.at[par, pl.ds(4, 2), rows], mp.at[par, pl.ds(lx + 4, 2), rows], "low outer")
+            add("gx", 1, 6, mp.at[par, pl.ds(lx, 2), rows], mp.at[par, pl.ds(0, 2), rows], "high inner")
+            add("gx", -1, 7, mp.at[par, pl.ds(6, 2), rows], mp.at[par, pl.ds(lx + 6, 2), rows], "low inner")
         if sizes["ga"] > 1:
             add("ga", 1, 2, yp.at[par, 0], yr.at[par, 0])
             add("ga", -1, 3, yp.at[par, 1], yr.at[par, 1])
@@ -412,7 +498,8 @@
         turned = pltpu.roll(m, (8 * x + 4) % lz, 1)
         return jnp.where((lane >= 8 * x) & (lane < 8 * x + 8), turned, packed), edges
 
-    order = list(range(4)) + list(range(lx - 4, lx)) + list(range(4, lx - 4))
+    order = [lx - 2, lx - 1, 0, 1, lx - 4, lx - 3, 2, 3] + list(range(4, lx - 4))
+    leave = {1: "high outer", 3: "low outer", 5: "high inner", 7: "low inner"}
 
     hidden = dot(w1[...], feats[...])
     hidden = (hidden * sigmoid(hidden)).astype(BF16)
@@ -443,11 +530,12 @@
         first_vector = (right[x] + block) * scale
         basis[0, x] = first_vector
         packed, edges = publish(0, x, first_vector, packed, edges)
-        if n == 7:
-            halo_start(0, "gx")
+        if n in leave:
+            halo_start(0, leave[n])
     zp[0] = packed
     halo_start(0, "ga", "gz")
     grads[...] = jnp.zeros_like(grads)
+    small[...] = jnp.zeros_like(small)
     count_samples()
 
     def iteration(i, carry):
@@ -474,8 +562,8 @@
             even = even + weighed * v
             odd = odd + weighed * m
             packed, edges = publish(later, x, m, packed, edges)
-            if n == 7:
-                pl.when(more)(lambda: halo_start(later, "gx"))
+            if n in leave:
+                pl.when(more)(lambda: halo_start(later, leave[n]))
         zp[later] = packed
         pl.when(more)(lambda: halo_start(later, "ga", "gz"))
         eta[2 * i] = jnp.sum(even.reshape(ly // 8, 8, lz), axis=0)
@@ -490,8 +578,6 @@
     mine = lax.broadcasted_iota(jnp.int32, (count, lz), 0) == lax.broadcasted_iota(jnp.int32, (count, lz), 1)
     row = jnp.sum(jnp.where(mine, sums, 0.0), axis=0, keepdims=True)
     sum_start(0, row)
-    for stage in range(ITERS - tiles, 5):
-        gradient_stage(stage)
     for phase in range(1, len(phases)):
         sum_start(phase, sum_wait(phase - 1))
     row = sum_wait(len(phases) - 1)
@@ -508,8 +594,9 @@
             r = r + along_r[j] * v
         press[x] = p
         resid[x] = pre[x] * (r + along_r[ITERS] * basis[ITERS, x])
-    gradient_stage(5)
-    total_grads[...] = full[...]
+    gradient_stage(STAGES)
+    total_grads[: 2 * ch] = full[...]
+    total_grads[2 * ch :] = jnp.sum(small_third[...], axis=0)
     sums_sent()
 
 
@@ -525,18 +612,19 @@
             n *= sizes[a]
         slots += n
     nx, nz, na = (sizes[a] for a in ("gx", "gz", "ga"))
-    unit = 8 * nz * na
-    rows = w1.shape[0] + w2.shape[0] + w3.shape[0]
-    rows = (rows + unit - 1) // unit * unit
+    rows = w1.shape[0] + w2.shape[0]
+    few = (w3.shape[0] + 7) // 8 * 8
+    pair = 2 if nz % 2 == 0 else 1
+    nh = nz // pair
     share = rows // nz
     piece = share // na
     tiles = columns // TILE
-    copies = max(2 * (nz - 1) + 2 * (na - 1) + nx - 1, 1)
+    copies = 3 + 3 * (nh - 1) + 3 * (na - 1) + 2 * (nx - 1)
     field = pltpu.VMEM((lx, ly, lz), F32)
     vmem = pl.BlockSpec(memory_space=pltpu.VMEM)
     return pl.pallas_call(
         functools.partial(solve_kernel, sizes),
-        out_shape=[jax.ShapeDtypeStruct((lx, ly, lz), F32)] * 2 + [jax.ShapeDtypeStruct((rows, ch), F32)],
+        out_shape=[jax.ShapeDtypeStruct((lx, ly, lz), F32)] * 2 + [jax.ShapeDtypeStruct((rows + few, ch), F32)],
         in_specs=[vmem] * 3 + [pl.BlockSpec(memory_space=pl.ANY)] + [vmem] * 5,
         out_specs=[vmem] * 3,
         scratch_shapes=[
@@ -554,17 +642,22 @@
             pltpu.VMEM((tiles, ch, TILE), BF16),
             pltpu.VMEM((columns // 128, 128), F32),
             pltpu.VMEM((rows, ch), F32),
-            pltpu.VMEM((max(nz - 1, 1), share, ch), F32),
+            pltpu.VMEM((rows // pair, ch), F32),
+            pltpu.VMEM((rows // pair, ch), F32),
+            pltpu.VMEM((max(nh - 1, 1), share, ch), F32),
             pltpu.VMEM((share, ch), F32),
             pltpu.VMEM((max(na - 1, 1), piece, ch), F32),
             pltpu.VMEM((piece, ch), F32),
             pltpu.VMEM((nx, piece, ch), F32),
             pltpu.VMEM((rows, ch), F32),
+            pltpu.VMEM((4, few, ch), F32),
+            pltpu.VMEM((nh + na - 1, few, ch), F32),
+            pltpu.VMEM((nx, few, ch), F32),
             pltpu.SemaphoreType.DMA((tiles,)),
             pltpu.SemaphoreType.DMA((copies,)),
             pltpu.SemaphoreType.DMA((copies,)),
-            pltpu.SemaphoreType.DMA((2, 6)),
-            pltpu.SemaphoreType.DMA((2, 6)),
+            pltpu.SemaphoreType.DMA((2, 8)),
+            pltpu.SemaphoreType.DMA((2, 8)),
             pltpu.SemaphoreType.DMA((slots,)),
             pltpu.SemaphoreType.DMA((slots,)),
         ],

time: 70.4 us -> 72.4 us (1.028)
  Pallas kernels: 69.6 us -> 71 us
    pallas_call x1, Pallas kernels: 67.3 us -> 68.7 us  [pressure_solve(): pl.pallas_call(functools.partial(solve_kernel, sizes), out_shape=[jax.Sha...]
where the time goes in v2:
time: 72.4 us; the launch traced here: 71.6 us
  Pallas kernels  71 us (98%)
    pallas_call x1, Pallas kernels, pressure_solve(): pl.pallas_call(functools.partial(solve_kernel, sizes), out_shape=[jax.Sha...  68.7 us
    pallas_call x1, Pallas kernels, finish(): pl.pallas_call(finish_kernel, out_shape=[jax.ShapeDtypeStruct(press.shape...  2.24 us

profile of v2, /device:TPU:1, one launch (start us, length us, event | category | flops | bytes accessed | tf_op | source)
XLA Modules:
  0.0 71.6 jit_solution(9662515678577106753)
XLA Ops:
  0.6 68.7 %shard_map.128 = (f32[16,32,128]{2,1,0:T(8,128)}, f32[16,32,128]{2,1,0:T(8,128)}, f32[520,256]{1,0:T(8,128)}) custom-call(f32[16,32,128]{2,1,0:T(8,128)} %right.1, f32[16,32,128]{2,1,0:T(8,128)} %diag.1, bf16[256,128]{1,0:T(8,128)(2,1)} %feats.1, bf16[256,4096]{1,0:T(8,128)(2,1)} %bank.1, bf16[6,4096]{1,0:T(8,128)(2,1)} %target.1, s32[1,2048]{1,0:T(1,128)} %bitcast.1, ...), custom_call_target="tpu_custom_call" | custom-call | flops 60000000 | bytes 200000000 | tf_op jit(solution)/shard_map/pallas_call | solution.py:625
  69.4 2.2 %shard_map.129 = (f32[16,32,128]{2,1,0:T(8,128)}, f32[16,32,128]{2,1,0:T(8,128)}, f32[256,256]{1,0:T(8,128)}, f32[256,256]{1,0:T(8,128)}, f32[6,256]{1,0:T(8,128)}) custom-call(f32[16,32,128]{2,1,0:T(8,128)} %get-tuple-element.8.press_in, f32[16,32,128]{2,1,0:T(8,128)} %get-tuple-element.9.resid_in, f32[520,256]{1,0:T(8,128)} %get-tuple-element.10.grads), custom_call_target="tpu_custom_call" | custom-call | flops 1000000 | bytes 2000000 | tf_op jit(solution)/shard_map/pallas_call | solution.py:686

commit v3 on v2

--- a/solution.py
+++ b/solution.py
@@ -9,11 +9,10 @@
 
 EL = 8
 ITERS = 12
-TILE = 256
-TILES_AT_ONCE = 3
+TILE = 1024
 AXES = ("gx", "gz", "ga")
 ONE_PHASE = 64
-STAGES = 7
+STAGE_STEPS = (0, 1, 3, 5, 6, 8)
 
 taps = (1.6, -0.2, 8.0 / 315.0, -1.0 / 560.0)
 center = 3.0 * 205.0 / 72.0
@@ -46,33 +45,83 @@
     return combos[1:]
 
 
-def krylov_coefficients(mu):
-    n = len(mu) // 2
-    one = jnp.ones_like(mu[0])
-    rho, pi = dict(enumerate(mu)), dict(enumerate(mu))
-    r, p, x = [one], [one], []
+def renormalized(s, e):
+    r = s + e
+    return r, e - (r - s)
+
+
+def two_sum(a, b):
+    s = a + b
+    t = s - a
+    return s, (a - (s - t)) + (b - t)
+
+
+def pair_add(a, b):
+    s, e = two_sum(a[0], b[0])
+    return renormalized(s, e + (a[1] + b[1]))
+
+
+def pair_scale(a, c):
+    return a[0] * c, a[1] * c
+
+
+def halves(v):
+    t = v * 4097.0
+    high = t - (t - v)
+    return high, v - high
+
+
+def pair_mul(a, b):
+    p = a[0] * b[0]
+    (ah, al), (bh, bl) = halves(a[0]), halves(b[0])
+    e = ((ah * bh - p) + ah * bl + al * bh) + al * bl
+    return renormalized(p, e + (a[0] * b[1] + a[1] * b[0]))
+
+
+def pair_div(a, b):
+    q = a[0] / b[0]
+    rest = pair_add(a, pair_scale(pair_mul((q, jnp.zeros_like(q)), b), -1.0))
+    return renormalized(q, rest[0] / b[0])
+
+
+def krylov_coefficients(eta):
+    count, lanes = eta[0].shape
+    n = count // 2
+    size = (n + 2 + 7) // 8 * 8
+    row = lax.broadcasted_iota(jnp.int32, (count, lanes), 0)
+    place = lax.broadcasted_iota(jnp.int32, (size, lanes), 0)
+
+    def at(v, j):
+        return tuple(jnp.broadcast_to(part[j : j + 1], (1, lanes)) for part in v)
+
+    def wide(v):
+        return tuple(jnp.broadcast_to(part, (count, lanes)) for part in v)
+
+    low = tuple(jnp.where(row % 2 == 0, e, o) for e, o in zip(wide(at(eta, 0)), wide(at(eta, 1))))
+    moments = pair_add(pair_scale(eta, 2.0), pair_scale(low, -1.0))
+    rho = tuple(jnp.where(row < 2, e, m) for e, m in zip(eta, moments))
+    pi = rho
+    r = jnp.where(place == 0, 1.0, 0.0)
+    p, x = r, jnp.zeros_like(r)
     for k in range(n):
-        last = 2 * n - 2 - k
-        tau = {}
-        for l in range(k, last + 1):
-            tau[l] = pi[l] + 0.5 * (pi[l + 1] + pi[abs(l - 1)])
-        alpha = rho[k] / tau[k]
-        x = [a + alpha * b for a, b in zip(x, p)] + [alpha * b for b in p[len(x):]]
-        moved = list(p) + [jnp.zeros_like(one)]
-        for j, b in enumerate(p):
-            if j == 0:
-                moved[1] = moved[1] + b
-            else:
-                moved[j - 1] = moved[j - 1] + 0.5 * b
-                moved[j + 1] = moved[j + 1] + 0.5 * b
-        r = [a - alpha * b for a, b in zip(r + [jnp.zeros_like(one)], moved)]
+        above = tuple(pltpu.roll(v, count - 1, 0) for v in pi)
+        below = tuple(pltpu.roll(v, 1, 0) for v in pi)
+        if k < 2:
+            below = tuple(jnp.where(row == 0, u, v) for u, v in zip(above, below))
+        tau = pair_add(pi, pair_scale(pair_add(above, below), 0.5))
+        alpha = pair_div(at(rho, k), at(tau, k))
+        step = jnp.broadcast_to(alpha[0], (size, lanes))
+        x = x + step * p
+        ahead = jnp.where(place < size - 1, pltpu.roll(p, size - 1, 0), 0.0)
+        r = r - step * (p + 0.5 * (ahead + pltpu.roll(jnp.where(place == 0, 2.0 * p, p), 1, 0)))
         if k + 1 < n:
-            new = {l: rho[l] - alpha * tau[l] for l in range(k + 1, last + 1)}
-            beta = (-alpha if k == 0 else -0.5 * alpha) * new[k + 1] / rho[k]
-            p = [a + beta * b for a, b in zip(r, p)] + r[len(p):]
-            pi = {l: (new[l] if l > k else 0.0) + beta * pi[l] for l in range(k, last + 1)}
+            new = pair_add(rho, pair_scale(pair_mul(wide(alpha), tau), -1.0))
+            gain = pair_scale(pair_div(at(new, k + 1), at(rho, k)), -1.0 if k == 0 else -0.5)
+            beta = pair_mul(alpha, gain)
+            p = r + jnp.broadcast_to(beta[0], (size, lanes)) * p
+            pi = pair_add(new, pair_mul(wide(beta), pi))
             rho = new
-    return [v * (1.0 / half) for v in x], r
+    return x * (1.0 / half), r
 
 
 def solve_kernel(
@@ -118,7 +167,9 @@
         for offs in shift_offsets([sizes[a] for a in axes]):
             to = {**pos, **coords(axes, offs, 1)}
             source = flat(axes, coords(axes, offs, -1))
-            peers.append((to, source))
+            far = sum(min(k, sizes[a] - k) for a, k in zip(axes, offs))
+            peers.append((far, to, source))
+        peers = [(to, source) for far, to, source in sorted(peers, key=lambda peer: -peer[0])]
         groups.append((me, peers))
 
     nx, nz, na = sizes["gx"], sizes["gz"], sizes["ga"]
@@ -318,18 +369,10 @@
         d1 = (dot(a2, d2, ((0,), (0,))) * (s1 * (1.0 + l1 * (1.0 - s1)))).astype(BF16)
         grads[:ch] += weighted(d1, x)
 
-    loops = -(-tiles // TILES_AT_ONCE)
-
     def gradient_work(i):
-        def one(t, carry):
-            gradient_tile(t)
-            return carry
-
-        lax.fori_loop(
-            jnp.minimum(i * TILES_AT_ONCE, tiles), jnp.minimum((i + 1) * TILES_AT_ONCE, tiles), one, 0
-        )
-        for stage in range(STAGES):
-            pl.when(i == min(loops - 1 + stage, ITERS - 1))(lambda stage=stage: gradient_stage(stage))
+        pl.when(i < tiles)(lambda: gradient_tile(i))
+        for stage, step in enumerate(STAGE_STEPS):
+            pl.when(i == tiles - 1 + step)(lambda stage=stage: gradient_stage(stage))
 
     mp[...] = jnp.zeros_like(mp)
     yr[...] = jnp.zeros_like(yr)
@@ -348,7 +391,7 @@
     def halo_copies(par):
         out = {}
 
-        def add(axis, step, number, src, dst, part=None):
+        def add(axis, step, number, src, dst):
             copy = pltpu.make_async_remote_copy(
                 src_ref=src,
                 dst_ref=dst,
@@ -359,14 +402,12 @@
             )
             can_send = pos[axis] < sizes[axis] - 1 if step > 0 else pos[axis] > 0
             will_get = pos[axis] > 0 if step > 0 else pos[axis] < sizes[axis] - 1
-            out.setdefault(part or axis, []).append((copy, can_send, will_get))
+            out.setdefault(axis, []).append((copy, can_send, will_get))
 
         rows = pl.ds(8, ly)
         if sizes["gx"] > 1:
-            add("gx", 1, 0, mp.at[par, pl.ds(lx + 2, 2), rows], mp.at[par, pl.ds(2, 2), rows], "high outer")
-            add("gx", -1, 1, mp.at[par, pl.ds(4, 2), rows], mp.at[par, pl.ds(lx + 4, 2), rows], "low outer")
-            add("gx", 1, 6, mp.at[par, pl.ds(lx, 2), rows], mp.at[par, pl.ds(0, 2), rows], "high inner")
-            add("gx", -1, 7, mp.at[par, pl.ds(6, 2), rows], mp.at[par, pl.ds(lx + 6, 2), rows], "low inner")
+            add("gx", 1, 0, mp.at[par, pl.ds(lx, 4), rows], mp.at[par, pl.ds(0, 4), rows])
+            add("gx", -1, 1, mp.at[par, pl.ds(4, 4), rows], mp.at[par, pl.ds(lx + 4, 4), rows])
         if sizes["ga"] > 1:
             add("ga", 1, 2, yp.at[par, 0], yr.at[par, 0])
             add("ga", -1, 3, yp.at[par, 1], yr.at[par, 1])
@@ -434,14 +475,24 @@
         count = len(groups[phase][1]) + 1
         for _, receive in sum_copies(phase):
             receive.wait_recv()
-        return jnp.sum(ar_dst[pl.ds(bases[phase], count)], axis=0)
+        parts = [ar_dst[bases[phase] + j] for j in range(count)]
+        parts = [(v, jnp.zeros_like(v)) for v in parts]
+        while len(parts) > 1:
+            joined = [pair_add(a, b) for a, b in zip(parts[::2], parts[1::2])]
+            parts = joined + parts[2 * len(joined) :]
+        return pair_add(parts[0], tuple(pltpu.roll(v, lz // 2, 1) for v in parts[0]))
+
+    def packed_pair(v):
+        first_half = lax.broadcasted_iota(jnp.int32, (1, lz), 1) < lz // 2
+        return jnp.where(first_half, v[0], pltpu.roll(v[1], lz // 2, 1))
 
     def sums_sent():
         for phase in range(len(phases)):
             for send, _ in sum_copies(phase):
                 send.wait_send()
 
-    def stencil_local(par):
+    def stencil_local(par, keep, start, back, older):
+        even = jnp.zeros((ly, lz), F32)
         for x in range(lx):
             v = mp[par, 4 + x, pl.ds(8, ly)]
             acc = None
@@ -455,7 +506,9 @@
                 t = t + jnp.where(lane < lz - k, pltpu.roll(v, lz - k, 1), 0.0)
                 t = taps[k - 1] * t
                 acc = t if acc is None else acc + t
-            nb[x] = acc
+            nb[x] = keep * v - start * (inv[x] * acc) - back * basis[older, x]
+            even = even + pre[x] * v * v
+        return even
 
     def z_correction(par):
         h = jnp.where(lane % 8 < 4, zr[par, 0], zr[par, 1])
@@ -467,15 +520,14 @@
             acc = acc + taps[k - 1] * (ahead + behind)
         return acc
 
-    def corrected(par, x, zc):
-        acc = nb[x]
+    def outer_part(par, x, zc):
+        z = pltpu.roll(zc, (2 * lz - 8 * x - 4) % lz, 1)
+        acc = jnp.where((lane < 4) | (lane >= lz - 4), z, 0.0)
         for k in range(1, 5):
             if x - k < 0:
                 acc = acc + taps[k - 1] * mp[par, 4 + x - k, pl.ds(8, ly)]
             if x + k >= lx:
                 acc = acc + taps[k - 1] * mp[par, 4 + x + k, pl.ds(8, ly)]
-        z = pltpu.roll(zc, (2 * lz - 8 * x - 4) % lz, 1)
-        acc = acc + jnp.where((lane < 4) | (lane >= lz - 4), z, 0.0)
         if x % 2 == 0:
             h = jnp.where(sub8 < 4, yr[par, 1, x // 2], yr[par, 0, x // 2])
         else:
@@ -498,8 +550,7 @@
         turned = pltpu.roll(m, (8 * x + 4) % lz, 1)
         return jnp.where((lane >= 8 * x) & (lane < 8 * x + 8), turned, packed), edges
 
-    order = [lx - 2, lx - 1, 0, 1, lx - 4, lx - 3, 2, 3] + list(range(4, lx - 4))
-    leave = {1: "high outer", 3: "low outer", 5: "high inner", 7: "low inner"}
+    order = list(range(4)) + list(range(lx - 4, lx)) + list(range(4, lx - 4))
 
     hidden = dot(w1[...], feats[...])
     hidden = (hidden * sigmoid(hidden)).astype(BF16)
@@ -530,8 +581,8 @@
         first_vector = (right[x] + block) * scale
         basis[0, x] = first_vector
         packed, edges = publish(0, x, first_vector, packed, edges)
-        if n in leave:
-            halo_start(0, leave[n])
+        if n == 7:
+            halo_start(0, "gx")
     zp[0] = packed
     halo_start(0, "ga", "gz")
     grads[...] = jnp.zeros_like(grads)
@@ -541,32 +592,27 @@
     def iteration(i, carry):
         par = lax.rem(i, 2)
         later = 1 - par
-        stencil_local(par)
+        start = jnp.where(i == 0, 0.5, 1.0)
+        back = jnp.where(i == 0, 0.0, 1.0)
+        keep = start * (2.0 / half - 2.0)
+        even = stencil_local(par, keep, start, back, jnp.maximum(i - 1, 0))
+        eta[2 * i] = jnp.sum(even.reshape(ly // 8, 8, lz), axis=0)
         gradient_work(i)
         halo_wait(par)
         zc = z_correction(par)
-        start = jnp.where(i == 0, 0.5, 1.0)
-        back = jnp.where(i == 0, 0.0, 1.0)
-        keep = start * (2.0 / half - 2.0)
         more = i < ITERS - 1
         packed = jnp.zeros((ly, lz), F32)
-        even = jnp.zeros((ly, lz), F32)
         odd = jnp.zeros((ly, lz), F32)
         edges = None
-        older = jnp.maximum(i - 1, 0)
         for n, x in enumerate(order):
-            v = mp[par, 4 + x, pl.ds(8, ly)]
-            m = keep * v - start * (inv[x] * corrected(par, x, zc)) - back * basis[older, x]
+            m = nb[x] - start * (inv[x] * outer_part(par, x, zc))
             basis[i + 1, x] = m
-            weighed = pre[x] * v
-            even = even + weighed * v
-            odd = odd + weighed * m
+            odd = odd + pre[x] * mp[par, 4 + x, pl.ds(8, ly)] * m
             packed, edges = publish(later, x, m, packed, edges)
-            if n in leave:
-                pl.when(more)(lambda: halo_start(later, leave[n]))
+            if n == 7:
+                pl.when(more)(lambda: halo_start(later, "gx"))
         zp[later] = packed
         pl.when(more)(lambda: halo_start(later, "ga", "gz"))
-        eta[2 * i] = jnp.sum(even.reshape(ly // 8, 8, lz), axis=0)
         eta[2 * i + 1] = jnp.sum(odd.reshape(ly // 8, 8, lz), axis=0)
         halo_sent(par)
         return carry
@@ -574,17 +620,27 @@
     lax.fori_loop(0, ITERS, iteration, 0)
 
     count = 2 * ITERS
-    sums = jnp.sum(jnp.sum(eta[...], axis=1), axis=1, keepdims=True)
+    lanes = jnp.sum(eta[...], axis=1)
+    coarse = jnp.max(jnp.abs(lanes), axis=1, keepdims=True) * (2.0 * lz)
+    upper = (lanes + coarse) - coarse
     mine = lax.broadcasted_iota(jnp.int32, (count, lz), 0) == lax.broadcasted_iota(jnp.int32, (count, lz), 1)
-    row = jnp.sum(jnp.where(mine, sums, 0.0), axis=0, keepdims=True)
+    row = packed_pair(
+        [
+            jnp.sum(jnp.where(mine, jnp.sum(v, axis=1, keepdims=True), 0.0), axis=0, keepdims=True)
+            for v in (upper, lanes - upper)
+        ]
+    )
     sum_start(0, row)
     for phase in range(1, len(phases)):
-        sum_start(phase, sum_wait(phase - 1))
-    row = sum_wait(len(phases) - 1)
-    spread_row = jnp.sum(jnp.where(mine, row, 0.0), axis=1, keepdims=True)
-    moment = [jnp.broadcast_to(spread_row[j : j + 1], (1, lz)) for j in range(count)]
-    mu = moment[:2] + [2.0 * moment[j] - moment[j % 2] for j in range(2, count)]
-    along_x, along_r = krylov_coefficients(mu)
+        sum_start(phase, packed_pair(sum_wait(phase - 1)))
+    sums = sum_wait(len(phases) - 1)
+    gradient_stage(6)
+    sums = tuple(
+        jnp.broadcast_to(jnp.sum(jnp.where(mine, v, 0.0), axis=1, keepdims=True), (count, lz)) for v in sums
+    )
+    in_x, in_r = krylov_coefficients(sums)
+    along_x = [jnp.broadcast_to(in_x[j : j + 1], (ly, lz)) for j in range(ITERS)]
+    along_r = [jnp.broadcast_to(in_r[j : j + 1], (ly, lz)) for j in range(ITERS + 1)]
     for x in range(lx):
         p = along_x[0] * basis[0, x]
         r = along_r[0] * basis[0, x]
@@ -594,7 +650,7 @@
             r = r + along_r[j] * v
         press[x] = p
         resid[x] = pre[x] * (r + along_r[ITERS] * basis[ITERS, x])
-    gradient_stage(STAGES)
+    gradient_stage(7)
     total_grads[: 2 * ch] = full[...]
     total_grads[2 * ch :] = jnp.sum(small_third[...], axis=0)
     sums_sent()
@@ -624,7 +680,7 @@
     vmem = pl.BlockSpec(memory_space=pltpu.VMEM)
     return pl.pallas_call(
         functools.partial(solve_kernel, sizes),
-        out_shape=[jax.ShapeDtypeStruct((lx, ly, lz), F32)] * 2 + [jax.ShapeDtypeStruct((rows + few, ch), F32)],
+        out_shape=[pltpu.VMEM((lx, ly, lz), F32)] * 2 + [pltpu.VMEM((rows + few, ch), F32)],
         in_specs=[vmem] * 3 + [pl.BlockSpec(memory_space=pl.ANY)] + [vmem] * 5,
         out_specs=[vmem] * 3,
         scratch_shapes=[
@@ -656,8 +712,8 @@
             pltpu.SemaphoreType.DMA((tiles,)),
             pltpu.SemaphoreType.DMA((copies,)),
             pltpu.SemaphoreType.DMA((copies,)),
-            pltpu.SemaphoreType.DMA((2, 8)),
-            pltpu.SemaphoreType.DMA((2, 8)),
+            pltpu.SemaphoreType.DMA((2, 6)),
+            pltpu.SemaphoreType.DMA((2, 6)),
             pltpu.SemaphoreType.DMA((slots,)),
             pltpu.SemaphoreType.DMA((slots,)),
         ],
@@ -690,7 +746,7 @@
         in_specs=[vmem] * 3,
         out_specs=[vmem] * 5,
         cost_estimate=pl.CostEstimate(flops=1_000_000, bytes_accessed=2_000_000, transcendentals=0),
-    )(press, resid, grads)
+    )(*(pltpu.with_memory_space_constraint(v, pltpu.VMEM) for v in (press, resid, grads)))
 
 
 def body(

time: 72.4 us -> 62.1 us (0.86)
  Pallas kernels: 71 us -> 60.6 us
    pallas_call x1, Pallas kernels: 68.7 us -> 59.5 us  [pressure_solve(): pl.pallas_call(functools.partial(solve_kernel, sizes), out_shape=[pltpu.V...]
    pallas_call x1, Pallas kernels: 2.24 us -> 1.04 us  [finish(): pl.pallas_call(finish_kernel, out_shape=[jax.ShapeDtypeStruct(press.shape...]
where the time goes in v3:
time: 62.1 us; the launch traced here: 61.2 us
  Pallas kernels  60.6 us (98%)
  between operations  0.64 us (1%)
    pallas_call x1, Pallas kernels, pressure_solve(): pl.pallas_call(functools.partial(solve_kernel, sizes), out_shape=[pltpu.V...  59.5 us

profile of v3, /device:TPU:1, one launch (start us, length us, event | category | flops | bytes accessed | tf_op | source)
XLA Modules:
  0.0 61.2 jit_solution(16755578314866719973)
XLA Ops:
  0.6 59.5 %shard_map.128 = (f32[16,32,128]{2,1,0:T(8,128)S(1)}, f32[16,32,128]{2,1,0:T(8,128)S(1)}, f32[520,256]{1,0:T(8,128)S(1)}) custom-call(f32[16,32,128]{2,1,0:T(8,128)} %right.1, f32[16,32,128]{2,1,0:T(8,128)} %diag.1, bf16[256,128]{1,0:T(8,128)(2,1)} %feats.1, bf16[256,4096]{1,0:T(8,128)(2,1)} %bank.1, bf16[6,4096]{1,0:T(8,128)(2,1)} %target.1, ...), custom_call_target="tpu_custom_call" | custom-call | flops 60000000 | bytes 200000000 | tf_op jit(solution)/shard_map/pallas_call | solution.py:681
  60.2 1.0 %shard_map.129 = (f32[16,32,128]{2,1,0:T(8,128)}, f32[16,32,128]{2,1,0:T(8,128)}, f32[256,256]{1,0:T(8,128)}, f32[256,256]{1,0:T(8,128)}, f32[6,256]{1,0:T(8,128)}) custom-call(f32[16,32,128]{2,1,0:T(8,128)S(1)} %get-tuple-element.8.press_in, f32[16,32,128]{2,1,0:T(8,128)S(1)} %get-tuple-element.9.resid_in, f32[520,256]{1,0:T(8,128)S(1)} %get-tuple-element.10.grads), custom_call_target="tpu_custom_call" | custom-call | flops 1000000 | bytes 2000000 | tf_op jit(solution)/shard_map/pallas_call | solution.py:742

commit v4 on v3

--- a/solution.py
+++ b/solution.py
@@ -12,7 +12,7 @@
 TILE = 1024
 AXES = ("gx", "gz", "ga")
 ONE_PHASE = 64
-STAGE_STEPS = (0, 1, 3, 5, 6, 8)
+STAGE_STEPS = (1, 2, 4, 6, 7, 8)
 
 taps = (1.6, -0.2, 8.0 / 315.0, -1.0 / 560.0)
 center = 3.0 * 205.0 / 72.0
@@ -71,17 +71,16 @@
     return high, v - high
 
 
-def pair_mul(a, b):
-    p = a[0] * b[0]
-    (ah, al), (bh, bl) = halves(a[0]), halves(b[0])
-    e = ((ah * bh - p) + ah * bl + al * bh) + al * bl
-    return renormalized(p, e + (a[0] * b[1] + a[1] * b[0]))
-
-
-def pair_div(a, b):
-    q = a[0] / b[0]
-    rest = pair_add(a, pair_scale(pair_mul((q, jnp.zeros_like(q)), b), -1.0))
-    return renormalized(q, rest[0] / b[0])
+def product(a, b, parts):
+    p = a * b
+    (ah, al), (bh, bl) = parts, halves(b)
+    return p, ((ah * bh - p) + ah * bl + al * bh) + al * bl
+
+
+def pair_div(a, b, inverse):
+    q = a[0] * inverse
+    p, e = product(q, b[0], halves(q))
+    return renormalized(q, (((a[0] - p) - e) + (a[1] - q * b[1])) * inverse)
 
 
 def krylov_coefficients(eta):
@@ -96,6 +95,12 @@
 
     def wide(v):
         return tuple(jnp.broadcast_to(part, (count, lanes)) for part in v)
+
+    def plus_product(a, c, v):
+        c0, c1 = wide(c)
+        p, e = product(c0, v[0], wide(halves(c[0])))
+        value, error = two_sum(a[0], p)
+        return renormalized(value, error + (a[1] + (e + (c0 * v[1] + c1 * v[0]))))
 
     low = tuple(jnp.where(row % 2 == 0, e, o) for e, o in zip(wide(at(eta, 0)), wide(at(eta, 1))))
     moments = pair_add(pair_scale(eta, 2.0), pair_scale(low, -1.0))
@@ -108,29 +113,39 @@
         below = tuple(pltpu.roll(v, 1, 0) for v in pi)
         if k < 2:
             below = tuple(jnp.where(row == 0, u, v) for u, v in zip(above, below))
-        tau = pair_add(pi, pair_scale(pair_add(above, below), 0.5))
-        alpha = pair_div(at(rho, k), at(tau, k))
+        near, rest = two_sum(above[0], below[0])
+        value, error = two_sum(pi[0], 0.5 * near)
+        tau = value, error + (pi[1] + 0.5 * (rest + (above[1] + below[1])))
+        pivot = at(tau, k)
+        inverse = 1.0 / pivot[0]
+        alpha = pair_div(at(rho, k), pivot, inverse)
         step = jnp.broadcast_to(alpha[0], (size, lanes))
         x = x + step * p
         ahead = jnp.where(place < size - 1, pltpu.roll(p, size - 1, 0), 0.0)
         r = r - step * (p + 0.5 * (ahead + pltpu.roll(jnp.where(place == 0, 2.0 * p, p), 1, 0)))
         if k + 1 < n:
-            new = pair_add(rho, pair_scale(pair_mul(wide(alpha), tau), -1.0))
-            gain = pair_scale(pair_div(at(new, k + 1), at(rho, k)), -1.0 if k == 0 else -0.5)
-            beta = pair_mul(alpha, gain)
+            new = plus_product(rho, pair_scale(alpha, -1.0), tau)
+            beta = pair_scale(pair_div(at(new, k + 1), pivot, inverse), -1.0 if k == 0 else -0.5)
             p = r + jnp.broadcast_to(beta[0], (size, lanes)) * p
-            pi = pair_add(new, pair_mul(wide(beta), pi))
+            pi = plus_product(new, beta, pi)
             rho = new
     return x * (1.0 / half), r
 
 
 def solve_kernel(
-    sizes, right, diag, feats, bank, target, index, w1, w2, w3, press, resid, total_grads,
+    sizes, right_in, diag_in, feats_in, bank, target_in, index_in, w1_in, w2_in, w3_in, press, resid, total_grads,
+    right, diag, feats, target, index, w1, w2, w3, in_sem,
     mp, nb, basis, pre, inv, yp, yr, zp, zr, eta, ar_src, ar_dst,
     bank_v, counts, grads, swapped, halved, first, held, second, owned, third, full,
     small, small_in, small_third,
     bank_sem, g_send, g_recv, h_send, h_recv, a_send, a_recv,
 ):
+    given = ((feats_in, feats), (w1_in, w1), (w2_in, w2), (w3_in, w3), (diag_in, diag), (right_in, right),
+             (index_in, index), (target_in, target))
+    given = [pltpu.make_async_copy(src, dst, in_sem.at[n]) for n, (src, dst) in enumerate(given)]
+    for copy in given:
+        copy.start()
+
     lx, ly, lz = right.shape
     ch, columns = bank.shape
     stress = target.shape[0]
@@ -422,9 +437,10 @@
             for copy, can_send, _ in copies.get(axis, []):
                 pl.when(can_send)(copy.start)
 
-    def halo_wait(par):
-        for copies in halo_copies(par).values():
-            for copy, _, will_get in copies:
+    def halo_wait(par, *axes):
+        copies = halo_copies(par)
+        for axis in axes:
+            for copy, _, will_get in copies.get(axis, []):
                 pl.when(will_get)(copy.wait_recv)
 
     def halo_sent(par):
@@ -520,14 +536,9 @@
             acc = acc + taps[k - 1] * (ahead + behind)
         return acc
 
-    def outer_part(par, x, zc):
+    def side_part(par, x, zc):
         z = pltpu.roll(zc, (2 * lz - 8 * x - 4) % lz, 1)
         acc = jnp.where((lane < 4) | (lane >= lz - 4), z, 0.0)
-        for k in range(1, 5):
-            if x - k < 0:
-                acc = acc + taps[k - 1] * mp[par, 4 + x - k, pl.ds(8, ly)]
-            if x + k >= lx:
-                acc = acc + taps[k - 1] * mp[par, 4 + x + k, pl.ds(8, ly)]
         if x % 2 == 0:
             h = jnp.where(sub8 < 4, yr[par, 1, x // 2], yr[par, 0, x // 2])
         else:
@@ -540,6 +551,15 @@
         parts = [acc[:8] + low] + ([acc[8:-8]] if ly > 16 else []) + [acc[-8:] + high]
         return jnp.concatenate(parts, axis=0)
 
+    def end_part(par, x):
+        acc = None
+        for k in range(1, 5):
+            for at in (4 + x - k, 4 + x + k):
+                if at < 4 or at >= lx + 4:
+                    t = taps[k - 1] * mp[par, at, pl.ds(8, ly)]
+                    acc = t if acc is None else acc + t
+        return acc
+
     def publish(par, x, m, packed, edges):
         mp[par, 4 + x, pl.ds(8, ly)] = m
         if x % 2 == 0:
@@ -550,8 +570,11 @@
         turned = pltpu.roll(m, (8 * x + 4) % lz, 1)
         return jnp.where((lane >= 8 * x) & (lane < 8 * x + 8), turned, packed), edges
 
-    order = list(range(4)) + list(range(lx - 4, lx)) + list(range(4, lx - 4))
-
+    ends = list(range(4)) + list(range(lx - 4, lx))
+    inner = list(range(4, lx - 4))
+
+    for copy in given[:4]:
+        copy.wait()
     hidden = dot(w1[...], feats[...])
     hidden = (hidden * sigmoid(hidden)).astype(BF16)
     hidden = dot(w2[...], hidden)
@@ -568,10 +591,12 @@
         [trace if e == 0 else pltpu.roll(trace, (lz - e * ez) % lz, 1) for e in range(ex * ey)], axis=0
     )
     forcing = dot(lines, spread, precision=lax.Precision.HIGHEST)
+    for copy in given[4:6]:
+        copy.wait()
     pl.semaphore_wait(barrier, total)
     packed = jnp.zeros((ly, lz), F32)
     edges = None
-    for n, x in enumerate(order):
+    for n, x in enumerate(ends + inner):
         line = forcing[(x // EL) * ey : (x // EL) * ey + ey]
         block = jnp.concatenate([jnp.broadcast_to(line[j : j + 1], (EL, lz)) for j in range(ey)], axis=0)
         whole = diag[x] + center
@@ -587,6 +612,8 @@
     halo_start(0, "ga", "gz")
     grads[...] = jnp.zeros_like(grads)
     small[...] = jnp.zeros_like(small)
+    for copy in given[6:]:
+        copy.wait()
     count_samples()
 
     def iteration(i, carry):
@@ -598,19 +625,26 @@
         even = stencil_local(par, keep, start, back, jnp.maximum(i - 1, 0))
         eta[2 * i] = jnp.sum(even.reshape(ly // 8, 8, lz), axis=0)
         gradient_work(i)
-        halo_wait(par)
+        halo_wait(par, "ga", "gz")
         zc = z_correction(par)
         more = i < ITERS - 1
         packed = jnp.zeros((ly, lz), F32)
         odd = jnp.zeros((ly, lz), F32)
         edges = None
-        for n, x in enumerate(order):
-            m = nb[x] - start * (inv[x] * outer_part(par, x, zc))
+        for x in ends:
+            nb[x] = nb[x] - start * (inv[x] * side_part(par, x, zc))
+        for x in inner:
+            m = nb[x] - start * (inv[x] * side_part(par, x, zc))
             basis[i + 1, x] = m
             odd = odd + pre[x] * mp[par, 4 + x, pl.ds(8, ly)] * m
             packed, edges = publish(later, x, m, packed, edges)
-            if n == 7:
-                pl.when(more)(lambda: halo_start(later, "gx"))
+        halo_wait(par, "gx")
+        for x in ends:
+            m = nb[x] - start * (inv[x] * end_part(par, x))
+            basis[i + 1, x] = m
+            odd = odd + pre[x] * mp[par, 4 + x, pl.ds(8, ly)] * m
+            packed, edges = publish(later, x, m, packed, edges)
+        pl.when(more)(lambda: halo_start(later, "gx"))
         zp[later] = packed
         pl.when(more)(lambda: halo_start(later, "ga", "gz"))
         eta[2 * i + 1] = jnp.sum(odd.reshape(ly // 8, 8, lz), axis=0)
@@ -676,14 +710,17 @@
     piece = share // na
     tiles = columns // TILE
     copies = 3 + 3 * (nh - 1) + 3 * (na - 1) + 2 * (nx - 1)
+    inputs = (right_side, diagonal, feats, bank, target, index.reshape(1, -1), w1, w2, w3)
     field = pltpu.VMEM((lx, ly, lz), F32)
     vmem = pl.BlockSpec(memory_space=pltpu.VMEM)
     return pl.pallas_call(
         functools.partial(solve_kernel, sizes),
         out_shape=[pltpu.VMEM((lx, ly, lz), F32)] * 2 + [pltpu.VMEM((rows + few, ch), F32)],
-        in_specs=[vmem] * 3 + [pl.BlockSpec(memory_space=pl.ANY)] + [vmem] * 5,
+        in_specs=[pl.BlockSpec(memory_space=pl.ANY)] * 9,
         out_specs=[vmem] * 3,
-        scratch_shapes=[
+        scratch_shapes=[pltpu.VMEM(v.shape, v.dtype) for v in inputs if v is not bank]
+        + [
+            pltpu.SemaphoreType.DMA((len(inputs) - 1,)),
             pltpu.VMEM((2, lx + 8, ly + 16, lz), F32),
             field,
             pltpu.VMEM((ITERS + 1, lx, ly, lz), F32),
@@ -721,7 +758,7 @@
         cost_estimate=pl.CostEstimate(
             flops=60_000_000, bytes_accessed=200_000_000, transcendentals=0
         ),
-    )(right_side, diagonal, feats, bank, target, index.reshape(1, -1), w1, w2, w3)
+    )(*inputs)
 
 
 def finish_kernel(press_in, resid_in, grads, press, resid, step1, step2, step3):

time: 62.1 us -> 58.9 us (0.948)
  Pallas kernels: 60.6 us -> 57.9 us
    pallas_call x1, Pallas kernels: 59.5 us -> 56.8 us  [pressure_solve(): pl.pallas_call(functools.partial(solve_kernel, sizes), out_shape=[pltpu.V...]
where the time goes in v4:
time: 58.9 us; the launch traced here: 58.5 us
  Pallas kernels  57.9 us (98%)
  between operations  0.64 us (1%)
    pallas_call x1, Pallas kernels, pressure_solve(): pl.pallas_call(functools.partial(solve_kernel, sizes), out_shape=[pltpu.V...  56.8 us

profile of v4, /device:TPU:1, one launch (start us, length us, event | category | flops | bytes accessed | tf_op | source)
XLA Modules:
  0.0 58.5 jit_solution(14455934439868574931)
XLA Ops:
  0.6 56.8 %shard_map.128 = (f32[16,32,128]{2,1,0:T(8,128)S(1)}, f32[16,32,128]{2,1,0:T(8,128)S(1)}, f32[520,256]{1,0:T(8,128)S(1)}) custom-call(f32[16,32,128]{2,1,0:T(8,128)} %right_in.1, f32[16,32,128]{2,1,0:T(8,128)} %diag_in.1, bf16[256,128]{1,0:T(8,128)(2,1)} %feats_in.1, bf16[256,4096]{1,0:T(8,128)(2,1)} %bank.1, bf16[6,4096]{1,0:T(8,128)(2,1)} %target_in.1, ...), custom_call_target="tpu_custom_call" | custom-call | flops 60000000 | bytes 200000000 | tf_op jit(solution)/shard_map/pallas_call | solution.py:716
  57.5 1.0 %shard_map.129 = (f32[16,32,128]{2,1,0:T(8,128)}, f32[16,32,128]{2,1,0:T(8,128)}, f32[256,256]{1,0:T(8,128)}, f32[256,256]{1,0:T(8,128)}, f32[6,256]{1,0:T(8,128)}) custom-call(f32[16,32,128]{2,1,0:T(8,128)S(1)} %get-tuple-element.8.press_in, f32[16,32,128]{2,1,0:T(8,128)S(1)} %get-tuple-element.9.resid_in, f32[520,256]{1,0:T(8,128)S(1)} %get-tuple-element.10.grads), custom_call_target="tpu_custom_call" | custom-call | flops 1000000 | bytes 2000000 | tf_op jit(solution)/shard_map/pallas_call | solution.py:779

commit v5 on v4

--- a/solution.py
+++ b/solution.py
@@ -12,7 +12,7 @@
 TILE = 1024
 AXES = ("gx", "gz", "ga")
 ONE_PHASE = 64
-STAGE_STEPS = (1, 2, 4, 6, 7, 8)
+STAGE_STEPS = ((1, 1), (2, 3), (3, 4), (4, 5), (5, 6), (6, 7), (7, 8))
 
 taps = (1.6, -0.2, 8.0 / 315.0, -1.0 / 560.0)
 center = 3.0 * 205.0 / 72.0
@@ -306,9 +306,12 @@
                 total, few = total + first[k - 1], few + small_in[k]
             held[...] = total
             small[2] = few
-            for k in range(1, na):
+            for k in range(1, na, 2):
                 start(scatter_ga(k))
         elif stage == 3:
+            for k in range(2, na, 2):
+                start(scatter_ga(k))
+        elif stage == 4:
             total, few = held[pl.ds(pl.multiple_of(pos["ga"] * piece, 8), piece), :], small[2]
             for k in range(1, na):
                 arrived(scatter_ga(k))
@@ -319,18 +322,21 @@
             small_third[pos["gx"]] = few
             for k in range(1, nx):
                 start(add_gx(k))
-        elif stage == 4:
+        elif stage == 5:
             for k in range(1, nx):
                 arrived(add_gx(k, -1))
             full[block_of(spot, pos["ga"]), :] = jnp.sum(third[...], axis=0)
-            for k in range(1, na):
+            for k in range(1, na, 2):
                 start(gather_ga(k))
-        elif stage == 5:
+        elif stage == 6:
+            for k in range(2, na, 2):
+                start(gather_ga(k))
+        elif stage == 7:
             for k in range(1, na):
                 arrived(gather_ga(k, -1))
             for k in range(1, nh):
                 start(gather_gz(k))
-        elif stage == 6:
+        elif stage == 8:
             for k in range(1, nh):
                 arrived(gather_gz(k, -1))
             if pair > 1:
@@ -384,10 +390,18 @@
         d1 = (dot(a2, d2, ((0,), (0,))) * (s1 * (1.0 + l1 * (1.0 - s1)))).astype(BF16)
         grads[:ch] += weighted(d1, x)
 
+    def gradient_exchange(i):
+        for stage, step in STAGE_STEPS:
+            pl.when(i == tiles - 1 + step)(lambda stage=stage: gradient_stage(stage))
+
     def gradient_work(i):
-        pl.when(i < tiles)(lambda: gradient_tile(i))
-        for stage, step in enumerate(STAGE_STEPS):
-            pl.when(i == tiles - 1 + step)(lambda stage=stage: gradient_stage(stage))
+        @pl.when(i < tiles)
+        def _():
+            gradient_tile(i)
+
+            @pl.when(i == tiles - 1)
+            def _():
+                gradient_stage(0)
 
     mp[...] = jnp.zeros_like(mp)
     yr[...] = jnp.zeros_like(yr)
@@ -622,6 +636,7 @@
         start = jnp.where(i == 0, 0.5, 1.0)
         back = jnp.where(i == 0, 0.0, 1.0)
         keep = start * (2.0 / half - 2.0)
+        gradient_exchange(i)
         even = stencil_local(par, keep, start, back, jnp.maximum(i - 1, 0))
         eta[2 * i] = jnp.sum(even.reshape(ly // 8, 8, lz), axis=0)
         gradient_work(i)
@@ -668,7 +683,7 @@
     for phase in range(1, len(phases)):
         sum_start(phase, packed_pair(sum_wait(phase - 1)))
     sums = sum_wait(len(phases) - 1)
-    gradient_stage(6)
+    gradient_stage(8)
     sums = tuple(
         jnp.broadcast_to(jnp.sum(jnp.where(mine, v, 0.0), axis=1, keepdims=True), (count, lz)) for v in sums
     )
@@ -684,7 +699,7 @@
             r = r + along_r[j] * v
         press[x] = p
         resid[x] = pre[x] * (r + along_r[ITERS] * basis[ITERS, x])
-    gradient_stage(7)
+    gradient_stage(9)
     total_grads[: 2 * ch] = full[...]
     total_grads[2 * ch :] = jnp.sum(small_third[...], axis=0)
     sums_sent()

time: 58.9 us -> 58.2 us (0.988)
  Pallas kernels: 57.9 us -> 57.1 us
    pallas_call x1, Pallas kernels: 56.8 us -> 56.1 us  [pressure_solve(): pl.pallas_call(functools.partial(solve_kernel, sizes), out_shape=[pltpu.V...]
where the time goes in v5:
time: 58.2 us; the launch traced here: 57.8 us
  Pallas kernels  57.1 us (98%)
  between operations  0.64 us (1%)
    pallas_call x1, Pallas kernels, pressure_solve(): pl.pallas_call(functools.partial(solve_kernel, sizes), out_shape=[pltpu.V...  56.1 us

profile of v5, /device:TPU:1, one launch (start us, length us, event | category | flops | bytes accessed | tf_op | source)
XLA Modules:
  0.0 57.8 jit_solution(11954601162848108694)
XLA Ops:
  0.6 56.1 %shard_map.128 = (f32[16,32,128]{2,1,0:T(8,128)S(1)}, f32[16,32,128]{2,1,0:T(8,128)S(1)}, f32[520,256]{1,0:T(8,128)S(1)}) custom-call(f32[16,32,128]{2,1,0:T(8,128)} %right_in.1, f32[16,32,128]{2,1,0:T(8,128)} %diag_in.1, bf16[256,128]{1,0:T(8,128)(2,1)} %feats_in.1, bf16[256,4096]{1,0:T(8,128)(2,1)} %bank.1, bf16[6,4096]{1,0:T(8,128)(2,1)} %target_in.1, ...), custom_call_target="tpu_custom_call" | custom-call | flops 60000000 | bytes 200000000 | tf_op jit(solution)/shard_map/pallas_call | solution.py:731
  56.7 1.0 %shard_map.129 = (f32[16,32,128]{2,1,0:T(8,128)}, f32[16,32,128]{2,1,0:T(8,128)}, f32[256,256]{1,0:T(8,128)}, f32[256,256]{1,0:T(8,128)}, f32[6,256]{1,0:T(8,128)}) custom-call(f32[16,32,128]{2,1,0:T(8,128)S(1)} %get-tuple-element.8.press_in, f32[16,32,128]{2,1,0:T(8,128)S(1)} %get-tuple-element.9.resid_in, f32[520,256]{1,0:T(8,128)S(1)} %get-tuple-element.10.grads), custom_call_target="tpu_custom_call" | custom-call | flops 1000000 | bytes 2000000 | tf_op jit(solution)/shard_map/pallas_call | solution.py:794

commit v6 on v5

--- a/solution.py
+++ b/solution.py
@@ -85,16 +85,17 @@
 
 def krylov_coefficients(eta):
     count, lanes = eta[0].shape
+    low_row, rows = 0, count
     n = count // 2
     size = (n + 2 + 7) // 8 * 8
     row = lax.broadcasted_iota(jnp.int32, (count, lanes), 0)
     place = lax.broadcasted_iota(jnp.int32, (size, lanes), 0)
 
     def at(v, j):
-        return tuple(jnp.broadcast_to(part[j : j + 1], (1, lanes)) for part in v)
+        return tuple(jnp.broadcast_to(part[j - low_row : j - low_row + 1], (1, lanes)) for part in v)
 
     def wide(v):
-        return tuple(jnp.broadcast_to(part, (count, lanes)) for part in v)
+        return tuple(jnp.broadcast_to(part, (rows, lanes)) for part in v)
 
     def plus_product(a, c, v):
         c0, c1 = wide(c)
@@ -109,7 +110,12 @@
     r = jnp.where(place == 0, 1.0, 0.0)
     p, x = r, jnp.zeros_like(r)
     for k in range(n):
-        above = tuple(pltpu.roll(v, count - 1, 0) for v in pi)
+        keep = max(k - 1, 0) // 8 * 8
+        end = min((2 * n - 1 - k) // 8 * 8 + 8, low_row + rows)
+        if (keep, end - keep) != (low_row, rows):
+            rho, pi = (tuple(part[keep - low_row : end - low_row] for part in v) for v in (rho, pi))
+            low_row, rows = keep, end - keep
+        above = tuple(pltpu.roll(v, rows - 1, 0) for v in pi)
         below = tuple(pltpu.roll(v, 1, 0) for v in pi)
         if k < 2:
             below = tuple(jnp.where(row == 0, u, v) for u, v in zip(above, below))
@@ -133,7 +139,7 @@
 
 
 def solve_kernel(
-    sizes, right_in, diag_in, feats_in, bank, target_in, index_in, w1_in, w2_in, w3_in, press, resid, total_grads,
+    sizes, right_in, diag_in, feats_in, bank, target_in, index_in, w1_in, w2_in, w3_in, press, resid, step1, step2, step3,
     right, diag, feats, target, index, w1, w2, w3, in_sem,
     mp, nb, basis, pre, inv, yp, yr, zp, zr, eta, ar_src, ar_dst,
     bank_v, counts, grads, swapped, halved, first, held, second, owned, third, full,
@@ -540,17 +546,17 @@
             even = even + pre[x] * v * v
         return even
 
-    def z_correction(par):
+    def z_correction(par, weights):
         h = jnp.where(lane % 8 < 4, zr[par, 0], zr[par, 1])
         acc = jnp.zeros((ly, lz), F32)
         place = lane % 8
         for k in range(1, 5):
             ahead = jnp.where((place >= 4) & (place - 4 < k), pltpu.roll(h, k, 1), 0.0)
             behind = jnp.where((place < 4) & (place >= 4 - k), pltpu.roll(h, lz - k, 1), 0.0)
-            acc = acc + taps[k - 1] * (ahead + behind)
+            acc = acc + weights[k - 1] * (ahead + behind)
         return acc
 
-    def side_part(par, x, zc):
+    def side_part(par, x, zc, weights):
         z = pltpu.roll(zc, (2 * lz - 8 * x - 4) % lz, 1)
         acc = jnp.where((lane < 4) | (lane >= lz - 4), z, 0.0)
         if x % 2 == 0:
@@ -560,22 +566,23 @@
         low = jnp.zeros((8, lz), F32)
         high = jnp.zeros((8, lz), F32)
         for k in range(1, 5):
-            low = low + taps[k - 1] * jnp.where(sub8 < k, pltpu.roll(h, k, 0), 0.0)
-            high = high + taps[k - 1] * jnp.where(sub8 >= 8 - k, pltpu.roll(h, 8 - k, 0), 0.0)
+            low = low + weights[k - 1] * jnp.where(sub8 < k, pltpu.roll(h, k, 0), 0.0)
+            high = high + weights[k - 1] * jnp.where(sub8 >= 8 - k, pltpu.roll(h, 8 - k, 0), 0.0)
         parts = [acc[:8] + low] + ([acc[8:-8]] if ly > 16 else []) + [acc[-8:] + high]
         return jnp.concatenate(parts, axis=0)
 
-    def end_part(par, x):
+    def end_part(par, x, weights):
         acc = None
         for k in range(1, 5):
             for at in (4 + x - k, 4 + x + k):
                 if at < 4 or at >= lx + 4:
-                    t = taps[k - 1] * mp[par, at, pl.ds(8, ly)]
+                    t = weights[k - 1] * mp[par, at, pl.ds(8, ly)]
                     acc = t if acc is None else acc + t
         return acc
 
-    def publish(par, x, m, packed, edges):
-        mp[par, 4 + x, pl.ds(8, ly)] = m
+    def publish(par, x, m, packed, edges, store=True):
+        if store:
+            mp[par, 4 + x, pl.ds(8, ly)] = m
         if x % 2 == 0:
             edges = (m[:8], m[-8:])
         else:
@@ -600,11 +607,15 @@
         lax.broadcasted_iota(jnp.int32, (lz, lz), 0) == lax.broadcasted_iota(jnp.int32, (lz, lz), 1) // EL,
         1.0,
         0.0,
-    )
+    ).astype(BF16)
     lines = jnp.concatenate(
         [trace if e == 0 else pltpu.roll(trace, (lz - e * ez) % lz, 1) for e in range(ex * ey)], axis=0
     )
-    forcing = dot(lines, spread, precision=lax.Precision.HIGHEST)
+    parts, rest = [], lines
+    for _ in range(3):
+        parts.append(rest.astype(BF16))
+        rest = rest - parts[-1].astype(F32)
+    forcing = sum(dot(part, spread) for part in parts)
     for copy in given[4:6]:
         copy.wait()
     pl.semaphore_wait(barrier, total)
@@ -641,25 +652,28 @@
         eta[2 * i] = jnp.sum(even.reshape(ly // 8, 8, lz), axis=0)
         gradient_work(i)
         halo_wait(par, "ga", "gz")
-        zc = z_correction(par)
+        weights = [start * t for t in taps]
+        zc = z_correction(par, weights)
         more = i < ITERS - 1
         packed = jnp.zeros((ly, lz), F32)
         odd = jnp.zeros((ly, lz), F32)
         edges = None
         for x in ends:
-            nb[x] = nb[x] - start * (inv[x] * side_part(par, x, zc))
+            nb[x] = nb[x] - inv[x] * side_part(par, x, zc, weights)
         for x in inner:
-            m = nb[x] - start * (inv[x] * side_part(par, x, zc))
+            m = nb[x] - inv[x] * side_part(par, x, zc, weights)
             basis[i + 1, x] = m
             odd = odd + pre[x] * mp[par, 4 + x, pl.ds(8, ly)] * m
             packed, edges = publish(later, x, m, packed, edges)
         halo_wait(par, "gx")
         for x in ends:
-            m = nb[x] - start * (inv[x] * end_part(par, x))
+            mp[later, 4 + x, pl.ds(8, ly)] = nb[x] - inv[x] * end_part(par, x, weights)
+        pl.when(more)(lambda: halo_start(later, "gx"))
+        for x in ends:
+            m = mp[later, 4 + x, pl.ds(8, ly)]
             basis[i + 1, x] = m
             odd = odd + pre[x] * mp[par, 4 + x, pl.ds(8, ly)] * m
-            packed, edges = publish(later, x, m, packed, edges)
-        pl.when(more)(lambda: halo_start(later, "gx"))
+            packed, edges = publish(later, x, m, packed, edges, False)
         zp[later] = packed
         pl.when(more)(lambda: halo_start(later, "ga", "gz"))
         eta[2 * i + 1] = jnp.sum(odd.reshape(ly // 8, 8, lz), axis=0)
@@ -680,10 +694,15 @@
         ]
     )
     sum_start(0, row)
+    gradient_stage(8)
+    gradient_stage(9)
+    last = jnp.sum(small_third[...], axis=0)[:stress]
+    for out, value in ((step1, full[:ch]), (step2, full[ch:]), (step3, last)):
+        squares = jnp.sum(jnp.sum(value * value, axis=0, keepdims=True), axis=1, keepdims=True)
+        out[...] = value * lax.rsqrt(squares / (out.shape[0] * ch) + epsilon)
     for phase in range(1, len(phases)):
         sum_start(phase, packed_pair(sum_wait(phase - 1)))
     sums = sum_wait(len(phases) - 1)
-    gradient_stage(8)
     sums = tuple(
         jnp.broadcast_to(jnp.sum(jnp.where(mine, v, 0.0), axis=1, keepdims=True), (count, lz)) for v in sums
     )
@@ -699,9 +718,6 @@
             r = r + along_r[j] * v
         press[x] = p
         resid[x] = pre[x] * (r + along_r[ITERS] * basis[ITERS, x])
-    gradient_stage(9)
-    total_grads[: 2 * ch] = full[...]
-    total_grads[2 * ch :] = jnp.sum(small_third[...], axis=0)
     sums_sent()
 
 
@@ -730,9 +746,9 @@
     vmem = pl.BlockSpec(memory_space=pltpu.VMEM)
     return pl.pallas_call(
         functools.partial(solve_kernel, sizes),
-        out_shape=[pltpu.VMEM((lx, ly, lz), F32)] * 2 + [pltpu.VMEM((rows + few, ch), F32)],
+        out_shape=[pltpu.VMEM((lx, ly, lz), F32)] * 2 + [pltpu.VMEM(w.shape, F32) for w in (w1, w2, w3)],
         in_specs=[pl.BlockSpec(memory_space=pl.ANY)] * 9,
-        out_specs=[vmem] * 3,
+        out_specs=[vmem] * 5,
         scratch_shapes=[pltpu.VMEM(v.shape, v.dtype) for v in inputs if v is not bank]
         + [
             pltpu.SemaphoreType.DMA((len(inputs) - 1,)),
@@ -776,29 +792,21 @@
     )(*inputs)
 
 
-def finish_kernel(press_in, resid_in, grads, press, resid, step1, step2, step3):
-    press[...] = press_in[...]
-    resid[...] = resid_in[...]
-    ch = step1.shape[0]
-    start = 0
-    for out in (step1, step2, step3):
-        count = out.shape[0]
-        value = grads[start : start + count]
-        squares = jnp.sum(jnp.sum(value * value, axis=0, keepdims=True), axis=1, keepdims=True)
-        out[...] = value * lax.rsqrt(squares / (count * ch) + epsilon)
-        start += count
-
-
-def finish(press, resid, grads, weights):
+def finish_kernel(*refs):
+    half_way = len(refs) // 2
+    for src, dst in zip(refs[:half_way], refs[half_way:]):
+        dst[...] = src[...]
+
+
+def finish(values):
     vmem = pl.BlockSpec(memory_space=pltpu.VMEM)
     return pl.pallas_call(
         finish_kernel,
-        out_shape=[jax.ShapeDtypeStruct(press.shape, F32)] * 2
-        + [jax.ShapeDtypeStruct(w.shape, F32) for w in weights],
-        in_specs=[vmem] * 3,
-        out_specs=[vmem] * 5,
+        out_shape=[jax.ShapeDtypeStruct(v.shape, v.dtype) for v in values],
+        in_specs=[vmem] * len(values),
+        out_specs=[vmem] * len(values),
         cost_estimate=pl.CostEstimate(flops=1_000_000, bytes_accessed=2_000_000, transcendentals=0),
-    )(*(pltpu.with_memory_space_constraint(v, pltpu.VMEM) for v in (press, resid, grads)))
+    )(*(pltpu.with_memory_space_constraint(v, pltpu.VMEM) for v in values))
 
 
 def body(
@@ -808,7 +816,7 @@
     solved = pressure_solve(
         right_side, diagonal, element_features, sample_bank, target_bank, patch_index, *weights
     )
-    return tuple(finish(*solved, weights))
+    return tuple(finish(solved))
 
 
 def solution(mesh):

time: 58.2 us -> 57.8 us (level)
  Pallas kernels: 57.1 us -> 56.3 us
    pallas_call x1, Pallas kernels: 56.1 us -> 55.3 us  [pressure_solve(): pl.pallas_call(functools.partial(solve_kernel, sizes), out_shape=[pltpu.V...]
where the time goes in v6:
time: 57.8 us; the launch traced here: 56.9 us
  Pallas kernels  56.3 us (97%)
  between operations  0.64 us (1%)
    pallas_call x1, Pallas kernels, pressure_solve(): pl.pallas_call(functools.partial(solve_kernel, sizes), out_shape=[pltpu.V...  55.3 us

profile of v6, /device:TPU:1, one launch (start us, length us, event | category | flops | bytes accessed | tf_op | source)
XLA Modules:
  0.0 56.9 jit_solution(14334213972073908947)
XLA Ops:
  0.6 55.3 %shard_map.128 = (f32[16,32,128]{2,1,0:T(8,128)S(1)}, f32[16,32,128]{2,1,0:T(8,128)S(1)}, f32[256,256]{1,0:T(8,128)S(1)}, f32[256,256]{1,0:T(8,128)S(1)}, f32[6,256]{1,0:T(8,128)S(1)}) custom-call(f32[16,32,128]{2,1,0:T(8,128)} %right_in.1, f32[16,32,128]{2,1,0:T(8,128)} %diag_in.1, bf16[256,128]{1,0:T(8,128)(2,1)} %feats_in.1, bf16[256,4096]{1,0:T(8,128)(2,1)} %bank.1, ...), custom_call_target="tpu_custom_call" | custom-call | flops 60000000 | bytes 200000000 | tf_op jit(solution)/shard_map/pallas_call | solution.py:747
  55.9 1.0 %shard_map.129 = (f32[16,32,128]{2,1,0:T(8,128)}, f32[16,32,128]{2,1,0:T(8,128)}, f32[256,256]{1,0:T(8,128)}, f32[256,256]{1,0:T(8,128)}, f32[6,256]{1,0:T(8,128)}) custom-call(f32[16,32,128]{2,1,0:T(8,128)S(1)} %get-tuple-element.10.refs_0_, f32[16,32,128]{2,1,0:T(8,128)S(1)} %get-tuple-element.11.refs_1_, f32[256,256]{1,0:T(8,128)S(1)} %get-tuple-element.12.refs_2_, ...), custom_call_target="tpu_custom_call" | custom-call | flops 1000000 | bytes 2000000 | tf_op jit(solution)/shard_map/pallas_call | solution.py:803

commit v7 on v6

--- a/solution.py
+++ b/solution.py
@@ -12,6 +12,7 @@
 TILE = 1024
 AXES = ("gx", "gz", "ga")
 ONE_PHASE = 64
+PLAIN = 3
 STAGE_STEPS = ((1, 1), (2, 3), (3, 4), (4, 5), (5, 6), (6, 7), (7, 8))
 
 taps = (1.6, -0.2, 8.0 / 315.0, -1.0 / 560.0)
@@ -81,6 +82,12 @@
     q = a[0] * inverse
     p, e = product(q, b[0], halves(q))
     return renormalized(q, (((a[0] - p) - e) + (a[1] - q * b[1])) * inverse)
+
+
+def pair_sum(a, b, c):
+    near, rest = two_sum(b[0], c[0])
+    value, error = two_sum(a[0], 0.5 * near)
+    return value, error + (a[1] + 0.5 * (rest + (b[1] + c[1])))
 
 
 def krylov_coefficients(eta):
@@ -119,21 +126,29 @@
         below = tuple(pltpu.roll(v, 1, 0) for v in pi)
         if k < 2:
             below = tuple(jnp.where(row == 0, u, v) for u, v in zip(above, below))
-        near, rest = two_sum(above[0], below[0])
-        value, error = two_sum(pi[0], 0.5 * near)
-        tau = value, error + (pi[1] + 0.5 * (rest + (above[1] + below[1])))
+        if k >= n - PLAIN:
+            tau = (pi[0] + 0.5 * (above[0] + below[0]), None)
+        else:
+            tau = pair_sum(pi, above, below)
+        plain = tau[1] is None
+        if plain:
+            tau, rho, pi = tau[:1], rho[:1], pi[:1]
         pivot = at(tau, k)
         inverse = 1.0 / pivot[0]
-        alpha = pair_div(at(rho, k), pivot, inverse)
+        alpha = (at(rho, k)[0] * inverse,) if plain else pair_div(at(rho, k), pivot, inverse)
         step = jnp.broadcast_to(alpha[0], (size, lanes))
         x = x + step * p
         ahead = jnp.where(place < size - 1, pltpu.roll(p, size - 1, 0), 0.0)
         r = r - step * (p + 0.5 * (ahead + pltpu.roll(jnp.where(place == 0, 2.0 * p, p), 1, 0)))
         if k + 1 < n:
-            new = plus_product(rho, pair_scale(alpha, -1.0), tau)
-            beta = pair_scale(pair_div(at(new, k + 1), pivot, inverse), -1.0 if k == 0 else -0.5)
+            if plain:
+                new = (rho[0] - wide(alpha)[0] * tau[0],)
+                beta = (at(new, k + 1)[0] * inverse * -0.5,)
+            else:
+                new = plus_product(rho, pair_scale(alpha, -1.0), tau)
+                beta = pair_scale(pair_div(at(new, k + 1), pivot, inverse), -1.0 if k == 0 else -0.5)
             p = r + jnp.broadcast_to(beta[0], (size, lanes)) * p
-            pi = plus_product(new, beta, pi)
+            pi = (new[0] + wide(beta)[0] * pi[0],) if plain else plus_product(new, beta, pi)
             rho = new
     return x * (1.0 / half), r
 

time: 57.8 us -> 57.7 us (level)
  no operation moved by 1% of the time
where the time goes in v7:
time: 57.7 us; the launch traced here: 56.8 us
  Pallas kernels  56.2 us (97%)
  between operations  0.64 us (1%)
    pallas_call x1, Pallas kernels, pressure_solve(): pl.pallas_call(functools.partial(solve_kernel, sizes), out_shape=[pltpu.V...  55.2 us

profile of v7, /device:TPU:1, one launch (start us, length us, event | category | flops | bytes accessed | tf_op | source)
XLA Modules:
  0.0 56.8 jit_solution(17204271000429385653)
XLA Ops:
  0.6 55.2 %shard_map.128 = (f32[16,32,128]{2,1,0:T(8,128)S(1)}, f32[16,32,128]{2,1,0:T(8,128)S(1)}, f32[256,256]{1,0:T(8,128)S(1)}, f32[256,256]{1,0:T(8,128)S(1)}, f32[6,256]{1,0:T(8,128)S(1)}) custom-call(f32[16,32,128]{2,1,0:T(8,128)} %right_in.1, f32[16,32,128]{2,1,0:T(8,128)} %diag_in.1, bf16[256,128]{1,0:T(8,128)(2,1)} %feats_in.1, bf16[256,4096]{1,0:T(8,128)(2,1)} %bank.1, ...), custom_call_target="tpu_custom_call" | custom-call | flops 60000000 | bytes 200000000 | tf_op jit(solution)/shard_map/pallas_call | solution.py:762
  55.8 1.0 %shard_map.129 = (f32[16,32,128]{2,1,0:T(8,128)}, f32[16,32,128]{2,1,0:T(8,128)}, f32[256,256]{1,0:T(8,128)}, f32[256,256]{1,0:T(8,128)}, f32[6,256]{1,0:T(8,128)}) custom-call(f32[16,32,128]{2,1,0:T(8,128)S(1)} %get-tuple-element.10.refs_0_, f32[16,32,128]{2,1,0:T(8,128)S(1)} %get-tuple-element.11.refs_1_, f32[256,256]{1,0:T(8,128)S(1)} %get-tuple-element.12.refs_2_, ...), custom_call_target="tpu_custom_call" | custom-call | flops 1000000 | bytes 2000000 | tf_op jit(solution)/shard_map/pallas_call | solution.py:818
